TPU v7x, 128 devices: a whole 4x4x4 slice. The times are simulated.
128 devices in a mesh: seq: 16 (over z, y_lo, core), kv: 8 (over y_hi, x).
Axes of the slice: x: 4, y: 4 (y_hi: 2, y_lo: 2; y = y_hi * 2 + y_lo), z: 4, core: 2. Of those that a mesh axis runs over, the one named last changes fastest.
Arguments:
- queries: bfloat16 [4096, 64, 128], P('seq', 'kv'), may hold values from -8 to 8
- keys: bfloat16 [4096, 8, 128], P('seq', 'kv'), may hold values from -8 to 8
- values: bfloat16 [4096, 8, 128], P('seq', 'kv'), may hold values from -6 to 6
- q_map: bfloat16 [64, 128, 128], P('kv'), may hold values from -0.5 to 0.5
- k_map: bfloat16 [8, 128, 128], P('kv'), may hold values from -0.5 to 0.5
- block_pairs: int32 [272, 2], replicated, may hold values from 0 to 31, as said below
Outputs:
- q_step: float32 [64, 128, 128], P('kv')
- k_step: float32 [8, 128, 128], P('kv')
- loss: float32 [], replicated
Inputs may be any that keep to these rules, and one draw needn't show every extreme that they name: `block_pairs`: each row is a pair (query block, key block) of blocks of 128 tokens, the key block never after the query block; query block q appears with itself and with exactly q // 2 distinct earlier blocks; no pair appears twice.
All inputs are finite; a program needn't handle non-finite values.
Results may differ from a plain program's by a relative error of at most 0.015.
Values may be sent and summed in bfloat16 or wider, within the bound.
No kernel may reach another device: no remote copies, remote signals or barrier semaphores. Data moves between devices by JAX's collectives and lax.ppermute only.
A program may use at most 64 MiB of HBM per device.

v0:
```python
import math

import jax
import jax.numpy as jnp
from jax import lax
from jax.sharding import PartitionSpec as P

HIGHEST_PRECISION = lax.Precision.HIGHEST
FLOOR_SCORE = -1e30


def swapped(block, axis, apart):
    count = lax.axis_size(axis)
    route = []
    for low in range(count):
        high = low | 1 << apart
        if high != low and high < count:
            route += [(low, high), (high, low)]
    return lax.ppermute(block, axis, route)


def sent_together(arrays, axis, dim, along):
    ends, at = ([], 0)
    for a in arrays[:-1]:
        at += a.shape[along]
        ends.append(at)
    both = jnp.concatenate(arrays, axis=along)
    return tuple(jnp.split(lax.all_gather(both, axis, axis=dim, tiled=True), ends, axis=along))


def total_of_pieces(shard, axis):
    tiles = lax.all_gather(shard, axis).astype(jnp.float32)
    return tiles.sum(axis=0)


def sent_to_all(shard, axis):
    copies = jnp.broadcast_to(shard, (lax.axis_size(axis), *shard.shape))
    return lax.all_to_all(copies, axis, split_axis=0, concat_axis=0, tiled=True)


def over_copies(shard, axis):
    everything = sent_to_all(shard, axis)
    return jnp.sum(everything, axis=0)


def together(arrays, axis):
    vector, at, finished = (jnp.concatenate([a.reshape(-1) for a in arrays]), 0, [])
    running = over_copies(vector, axis)
    for a in arrays:
        finished.append(running[at : at + a.size].reshape(a.shape))
        at += a.size
    return tuple(finished)


def soft_pair(lifted):
    return jnp.concatenate(
        [jax.nn.softmax(lifted, axis=-1), jax.nn.softmax(-lifted, axis=-1)], axis=-1
    )


def back_features(softened, upstream):
    half_width = softened.shape[-1] // 2
    leading, trailing = (softened[..., :half_width], softened[..., half_width:])
    up_lead, up_trail = (upstream[..., :half_width], upstream[..., half_width:])
    return leading * (up_lead - jnp.sum(leading * up_lead, axis=-1, keepdims=True)) - trailing * (
        up_trail - jnp.sum(trailing * up_trail, axis=-1, keepdims=True)
    )


def fresh_state(row_count, head_count, head_width):
    return (
        jnp.full((row_count, head_count), FLOOR_SCORE, jnp.float32),
        jnp.zeros((row_count, head_count), jnp.float32),
        jnp.zeros((row_count, head_count, head_width), jnp.float32),
        jnp.zeros((row_count, head_count, head_width), jnp.float32),
        jnp.zeros((row_count, head_count), jnp.float32),
    )


def forward_slab(
    running, query_block, mapped_query, allowed, key_slab, value_slab, mapped_slab, scaling
):
    running_max, running_total, teacher_value, student_value, student_norm = running
    visible = allowed[:, None, :]
    scores = (
        jnp.einsum("thd,sd->ths", query_block, key_slab, preferred_element_type=jnp.float32)
        * scaling
    )
    scores = jnp.where(visible, scores, FLOOR_SCORE)
    new_max = jnp.maximum(running_max, jnp.max(scores, axis=-1))
    weights = jnp.where(visible, jnp.exp(scores - new_max[:, :, None]), 0.0)
    rescale = jnp.exp(running_max - new_max)
    running_total = running_total * rescale + jnp.sum(weights, axis=-1)
    teacher_value = teacher_value * rescale[:, :, None] + jnp.einsum(
        "ths,sd->thd", weights.astype(jnp.bfloat16), value_slab, preferred_element_type=jnp.float32
    )
    mixing = jnp.where(
        visible,
        jnp.einsum("thf,sf->ths", mapped_query, mapped_slab, preferred_element_type=jnp.float32),
        0.0,
    )
    student_norm = student_norm + jnp.sum(mixing, axis=-1)
    student_value = student_value + jnp.einsum(
        "ths,sd->thd", mixing.astype(jnp.bfloat16), value_slab, preferred_element_type=jnp.float32
    )
    return (new_max, running_total, teacher_value, student_value, student_norm)


def body(queries, keys, values, q_map, k_map, block_pairs):
    tokens_here = queries.shape[0]
    head_count = queries.shape[1]
    head_width = queries.shape[2]
    half_rows = tokens_here // 2
    seq_count = lax.axis_size("seq")
    kv_count = lax.axis_size("kv")
    position = lax.axis_index("seq")
    block_count = 2 * seq_count
    scaling = 1.0 / math.sqrt(head_width)
    key_rows = keys[:, 0, :]
    value_rows = values[:, 0, :]
    key_weight = k_map[0]
    feature_width = 2 * key_weight.shape[1]
    block_ids = jnp.arange(block_count, dtype=jnp.int32)
    hit_query = (block_pairs[:, 0:1] == block_ids[None, :]).astype(jnp.float32)
    hit_key = (block_pairs[:, 1:2] == block_ids[None, :]).astype(jnp.float32)
    pair_table = jnp.dot(hit_query.T, hit_key, precision=HIGHEST_PRECISION)
    early_block = queries[:half_rows]
    late_block = queries[half_rows:]
    top_bit = seq_count.bit_length() - 2
    late_block = swapped(late_block, "seq", top_bit)
    partner = (position + seq_count // 2) % seq_count
    late_id = 2 * partner + 1
    query_blocks = (early_block, late_block)
    query_ids = (2 * position, late_id)
    pair_rows = []
    query_spots = []
    soft_queries = []
    mapped_queries = []
    for number in range(2):
        selector = (block_ids == query_ids[number]).astype(jnp.float32)
        pair_rows.append(jnp.dot(selector, pair_table, precision=HIGHEST_PRECISION))
        query_spots.append(query_ids[number] * half_rows + jnp.arange(half_rows, dtype=jnp.int32))
        softened = soft_pair(
            jnp.einsum(
                "thd,hdf->thf", query_blocks[number], q_map, preferred_element_type=jnp.float32
            )
        )
        soft_queries.append(softened)
        mapped_queries.append(softened.astype(jnp.bfloat16))

    def listed_pairs(number, first_row, row_count):
        key_spots = first_row + jnp.arange(row_count, dtype=jnp.int32)
        selector = ((key_spots // half_rows)[:, None] == block_ids[None, :]).astype(jnp.float32)
        listed = jnp.dot(selector, pair_rows[number], precision=HIGHEST_PRECISION) > 0.5
        return (query_spots[number][:, None] >= key_spots[None, :]) & listed[None, :]

    start_states = (
        fresh_state(half_rows, head_count, head_width),
        fresh_state(half_rows, head_count, head_width),
    )
    pieces = sent_together((key_rows, value_rows), "seq", 0, 1)
    key_part = pieces[0]
    value_part = pieces[1]
    row_count = key_part.shape[0]
    slab_rows = math.gcd(row_count, max(512, tokens_here))

    def forward_turn(turn_index, running):
        offset = turn_index * slab_rows
        key_slab = lax.dynamic_slice_in_dim(key_part, offset, slab_rows, 0)
        value_slab = lax.dynamic_slice_in_dim(value_part, offset, slab_rows, 0)
        mapped_slab = soft_pair(
            jnp.dot(key_slab, key_weight, preferred_element_type=jnp.float32)
        ).astype(jnp.bfloat16)
        updated = []
        for number in range(2):
            allowed = listed_pairs(number, offset, slab_rows)

            def advance(current, number=number, allowed=allowed):
                return forward_slab(
                    current,
                    query_blocks[number],
                    mapped_queries[number],
                    allowed,
                    key_slab,
                    value_slab,
                    mapped_slab,
                    scaling,
                )

            updated.append(
                lax.cond(jnp.any(allowed), advance, lambda unchanged: unchanged, running[number])
            )
        return tuple(updated)

    states = lax.fori_loop(0, row_count // slab_rows, forward_turn, start_states)
    loss_part = jnp.zeros((), jnp.float32)
    grad_nums = []
    grad_norms = []
    for number in range(2):
        running_max, running_total, teacher_value, student_value, student_norm = states[number]
        teacher = teacher_value / running_total[:, :, None]
        student = student_value / student_norm[:, :, None]
        mismatch = student - teacher
        loss_part = loss_part + jnp.sum(mismatch * mismatch)
        upstream = 2.0 * mismatch
        grad_nums.append((upstream / student_norm[:, :, None]).astype(jnp.bfloat16))
        grad_norms.append(-jnp.sum(upstream * student, axis=-1) / student_norm)
    key_side = jnp.zeros((head_width, key_weight.shape[1]), jnp.float32)
    empty_grads = tuple(
        (jnp.zeros((half_rows, head_count, feature_width), jnp.float32) for number in range(2))
    )
    backward_key_part, backward_value_part = sent_together((key_rows, value_rows), "seq", 0, 1)
    row_count = backward_key_part.shape[0]
    backward_slab_rows = math.gcd(row_count, max(512, tokens_here))

    def backward_turn(turn_index, current):
        query_grads, side_acc = current
        offset = turn_index * backward_slab_rows
        key_slab = lax.dynamic_slice_in_dim(backward_key_part, offset, backward_slab_rows, 0)
        value_slab = lax.dynamic_slice_in_dim(backward_value_part, offset, backward_slab_rows, 0)
        soft_key = soft_pair(jnp.dot(key_slab, key_weight, preferred_element_type=jnp.float32))
        mapped_slab = soft_key.astype(jnp.bfloat16)
        key_grad = jnp.zeros((backward_slab_rows, feature_width), jnp.float32)
        updated = []
        for number in range(2):
            allowed = listed_pairs(number, offset, backward_slab_rows)

            def retreat(grads_pair, number=number, allowed=allowed):
                query_grad, slab_grad = grads_pair
                grad_mix = jnp.where(
                    allowed[:, None, :],
                    jnp.einsum(
                        "thd,sd->ths",
                        grad_nums[number],
                        value_slab,
                        preferred_element_type=jnp.float32,
                    )
                    + grad_norms[number][:, :, None],
                    0.0,
                ).astype(jnp.bfloat16)
                query_grad = query_grad + jnp.einsum(
                    "ths,sf->thf", grad_mix, mapped_slab, preferred_element_type=jnp.float32
                )
                slab_grad = slab_grad + jnp.einsum(
                    "ths,thf->sf",
                    grad_mix,
                    mapped_queries[number],
                    preferred_element_type=jnp.float32,
                )
                return (query_grad, slab_grad)

            query_grad, key_grad = lax.cond(
                jnp.any(allowed),
                retreat,
                lambda unchanged: unchanged,
                (query_grads[number], key_grad),
            )
            updated.append(query_grad)
        side_acc = side_acc + jnp.dot(
            key_slab.astype(jnp.float32).T,
            back_features(soft_key, key_grad),
            precision=HIGHEST_PRECISION,
        )
        return (tuple(updated), side_acc)

    query_grads, key_side = lax.fori_loop(
        0, row_count // backward_slab_rows, backward_turn, (empty_grads, key_side)
    )
    grad_key = key_side
    grad_query = jnp.zeros((head_count, head_width, key_weight.shape[1]), jnp.float32)
    for number in range(2):
        lift_grad = back_features(soft_queries[number], query_grads[number])
        grad_query = grad_query + jnp.einsum(
            "thd,thf->hdf",
            query_blocks[number].astype(jnp.float32),
            lift_grad,
            precision=HIGHEST_PRECISION,
        )
    grad_query, grad_key, loss_part = (
        total_of_pieces(grad_query.astype(jnp.bfloat16), "seq").astype(jnp.float32),
        total_of_pieces(grad_key.astype(jnp.bfloat16), "seq").astype(jnp.float32),
        total_of_pieces(loss_part.astype(jnp.bfloat16), "seq").astype(jnp.float32),
    )
    squared = jnp.sum(grad_query * grad_query) + jnp.sum(grad_key * grad_key)
    squared, loss_total = together((squared, loss_part), "kv")
    entries = (head_count + k_map.shape[0]) * kv_count * head_width * key_weight.shape[1]
    scaled_norm = jnp.sqrt(squared / entries + 1e-06)
    loss = loss_total / (tokens_here * seq_count * head_count * kv_count * head_width)
    return (grad_query / scaled_norm, (grad_key / scaled_norm)[None], loss)


def solution(mesh):
    placed = (
        P("seq", "kv", None),
        P("seq", "kv", None),
        P("seq", "kv", None),
        P("kv", None, None),
        P("kv", None, None),
        P(),
    )
    return jax.shard_map(
        body,
        mesh=mesh,
        in_specs=placed,
        out_specs=(P("kv", None, None), P("kv", None, None), P()),
        check_vma=False,
    )
```

profile of v0, /device:TPU:0, one launch (start us, length us, event | category | flops | bytes accessed | tf_op | source)
XLA Modules:
  0.0 385.1 jit_solution(14751534128396678938)
XLA Ops:
  7.2 1.6 pad_maximum_fusion.4
  10.0 4.1 %collective-permute-start = (bf16[128,8,128]{2,0,1:T(8,128)(2,1)S(1)}, bf16[128,8,128]{2,0,1:T(8,128)(2,1)S(1)}, u32[]{:S(2)}, u32[]{:S(2)}) collective-permute-start(bf16[128,8,128]{2,0,1:T(8,128)(2,1)S(1)} %copy.122), channel_id=1, source_target_pairs={{0,64},{64,0},{8,72},{72,8},{16,80},{80,16},{24,88},{88,24},{32,96... | collective-permute-start | bytes 786440 | tf_op jit(solution)/shard_map/ppermute | solution.py:19
  22.0 24.8 %all-gather.5.cloned.1.call-done = bf16[4096,256]{1,0:T(8,128)(2,1)} async-done(((bf16[256,256]{1,0:T(8,128)(2,1)}), bf16[4096,256]{1,0:T(8,128)(2,1)}) %all-gather.5.cloned.1.call-update) | async-done | bytes 2097168 | tf_op jit(solution)/shard_map/all_gather | solution.py:28
  46.8 2.7 fusion.160
  53.3 76.5 %while.57 = (s32[]{:T(128)}, f32[128,8]{0,1:T(8,128)S(1)}, f32[128,8]{0,1:T(8,128)}, f32[128,8,128]{2,0,1:T(8,128)S(1)}, f32[128,8,128]{2,0,1:T(8,128)}, /*index...) while((s32[]{:T(128)}, f32[128,8]{0,1:T(8,128)S(1)}, ...), condition=%wide.region_25.26_spmd.clone, body=%wide.region_8.25_spmd.clone.sunk | while | flops 1379904768 | bytes 41725120 | solution.py:195
  58.9 4.3 %conditional.13 = ((f32[128,8]{0,1:T(8,128)S(1)}, f32[128,8]{0,1:T(8,128)}, f32[128,8,128]{2,0,1:T(8,128)}, f32[128,8,128]{2,0,1:T(8,128)}, f32[128,8]{0,1:T(8,128)S(1)})) conditional(s32[]{:T(128)} %convert_element_type.159, (f32[128,8]{0,1:T(8,128)S(1)}, f32[128,8]{0,1:T(8,128)}, f32[128,8,128]{2,0,1:T(8,128)}, f32[128,8,128]{2,0,1:T(8,128)}, ...), branch_computations={%region_20.20_spmd, %region_21.24_spmd} | conditional | flops 680396800 | bytes 20693208 | solution.py:191
  63.8 4.4 %conditional.12 = ((f32[128,8]{0,1:T(8,128)S(1)}, f32[128,8]{0,1:T(8,128)}, f32[128,8,128]{2,0,1:T(8,128)S(1)}, f32[128,8,128]{2,0,1:T(8,128)}, f32[128,8]{0,1:T(8,128)S(1)})) conditional(s32[]{:T(128)} %convert_element_type.158, (f32[128,8]{0,1:T(8,128)S(1)}, f32[128,8]{0,1:T(8,128)}, f32[128,8,128]{2,0,1:T(8,128)S(1)}, ...), branch_computations={%region_14.14_spmd, %region_15.18_spmd} | conditional | flops 680396800 | bytes 18596028 | solution.py:191
  73.9 4.3 %conditional.13 = ((f32[128,8]{0,1:T(8,128)S(1)}, f32[128,8]{0,1:T(8,128)}, f32[128,8,128]{2,0,1:T(8,128)}, f32[128,8,128]{2,0,1:T(8,128)}, f32[128,8]{0,1:T(8,128)S(1)})) conditional(s32[]{:T(128)} %convert_element_type.159, (f32[128,8]{0,1:T(8,128)S(1)}, f32[128,8]{0,1:T(8,128)}, f32[128,8,128]{2,0,1:T(8,128)}, f32[128,8,128]{2,0,1:T(8,128)}, ...), branch_computations={%region_20.20_spmd, %region_21.24_spmd} | conditional | flops 680396800 | bytes 20693208 | solution.py:191
  84.5 4.3 %conditional.13 = ((f32[128,8]{0,1:T(8,128)S(1)}, f32[128,8]{0,1:T(8,128)}, f32[128,8,128]{2,0,1:T(8,128)}, f32[128,8,128]{2,0,1:T(8,128)}, f32[128,8]{0,1:T(8,128)S(1)})) conditional(s32[]{:T(128)} %convert_element_type.159, (f32[128,8]{0,1:T(8,128)S(1)}, f32[128,8]{0,1:T(8,128)}, f32[128,8,128]{2,0,1:T(8,128)}, f32[128,8,128]{2,0,1:T(8,128)}, ...), branch_computations={%region_20.20_spmd, %region_21.24_spmd} | conditional | flops 680396800 | bytes 20693208 | solution.py:191
  95.1 4.3 %conditional.13 = ((f32[128,8]{0,1:T(8,128)S(1)}, f32[128,8]{0,1:T(8,128)}, f32[128,8,128]{2,0,1:T(8,128)}, f32[128,8,128]{2,0,1:T(8,128)}, f32[128,8]{0,1:T(8,128)S(1)})) conditional(s32[]{:T(128)} %convert_element_type.159, (f32[128,8]{0,1:T(8,128)S(1)}, f32[128,8]{0,1:T(8,128)}, f32[128,8,128]{2,0,1:T(8,128)}, f32[128,8,128]{2,0,1:T(8,128)}, ...), branch_computations={%region_20.20_spmd, %region_21.24_spmd} | conditional | flops 680396800 | bytes 20693208 | solution.py:191
  105.8 4.3 %conditional.13 = ((f32[128,8]{0,1:T(8,128)S(1)}, f32[128,8]{0,1:T(8,128)}, f32[128,8,128]{2,0,1:T(8,128)}, f32[128,8,128]{2,0,1:T(8,128)}, f32[128,8]{0,1:T(8,128)S(1)})) conditional(s32[]{:T(128)} %convert_element_type.159, (f32[128,8]{0,1:T(8,128)S(1)}, f32[128,8]{0,1:T(8,128)}, f32[128,8,128]{2,0,1:T(8,128)}, f32[128,8,128]{2,0,1:T(8,128)}, ...), branch_computations={%region_20.20_spmd, %region_21.24_spmd} | conditional | flops 680396800 | bytes 20693208 | solution.py:191
  129.8 3.0 multiply_reduce_fusion.2
  137.0 115.8 %while.58 = (s32[]{:T(128)}, f32[128,8,256]{2,0,1:T(8,128)S(1)}, f32[128,8,256]{2,0,1:T(8,128)S(1)}, f32[128,128]{1,0:T(8,128)}, f32[32]{0:T(128)}, /*index=5*/b...) while((s32[]{:T(128)}, f32[128,8,256]{2,0,1:T(8,128)S(1)}, ...), condition=%wide.region_41.42_spmd.clone, body=%wide.region_28.41_spmd.clone.sunk | while | flops 1467029760 | bytes 25406264 | solution.py:266
  140.4 1.5 fusion.232
  143.4 3.0 conditional.14
  147.0 3.0 conditional.15
  162.2 3.0 conditional.15
  173.7 1.5 fusion.232
  177.4 3.0 conditional.15
  188.9 1.5 fusion.232
  192.6 3.0 conditional.15
  204.1 1.5 fusion.232
  207.9 3.0 conditional.15
  219.4 1.5 fusion.232
  231.6 1.5 fusion.232
  243.9 1.5 fusion.232
  254.2 1.6 multiply_reduce_fusion.6
  257.2 1.5 multiply_reduce_fusion.8
  264.3 68.6 %all-reduce = bf16[16]{0:T(256)(128)(2,1)S(1)} all-reduce(bf16[16]{0:T(256)(128)(2,1)S(1)} %dynamic-update-slice), channel_id=1, replica_groups=mesh['seq'=16,'kv'=8] {'seq'}, use_global_device_ids=true, to_apply=%add | all-reduce | flops 16 | bytes 64
  333.4 19.3 %all-gather.1 = bf16[2048,128]{1,0:T(8,128)(2,1)S(1)} all-gather(bf16[128,128]{1,0:T(8,128)(2,1)S(1)} %convert_element_type.127), channel_id=3, replica_groups=mesh['seq'=16,'kv'=8] {'seq'}, dimensions={0}, use_global_device_ids=true | all-gather | bytes 557056 | tf_op jit(solution)/shard_map/all_gather | solution.py:32
  353.5 3.0 convert_reduce_fusion
  359.4 14.1 %all_to_all.6 = f32[8,1,2]{2,1,0:T(1,128)S(1)} all-to-all(f32[8,1,2]{2,1,0:T(1,128)S(1)} %broadcast_in_dim.176), channel_id=1, replica_groups=mesh['seq'=16,'kv'=8] {'kv'}, dimensions={0} | all-to-all | bytes 128 | tf_op jit(solution)/shard_map/all_to_all | solution.py:38
  (554 shorter events, 188.6 us)
Async XLA Ops:
  7.2 8.0 %copy-start = (bf16[8,128,128]{2,1,0:T(8,128)(2,1)S(1)}, bf16[8,128,128]{2,1,0:T(8,128)(2,1)}, u32[]{:S(2)}) copy-start(bf16[8,128,128]{2,1,0:T(8,128)(2,1)} %param.21) | copy-start | bytes 786436
  7.2 39.6 %all-gather.5.cloned.1.call-start = ((), (), s32[]{:S(2)}) async-start(), calls=%async_computation.1 | async-start | bytes 2228224 | tf_op jit(solution)/shard_map/all_gather | solution.py:28
  8.8 344.6 %all-gather.7.cloned.1.call-start = ((), (), s32[]{:S(2)}) async-start(), calls=%async_computation.2 | async-start | bytes 4456448 | tf_op jit(solution)/shard_map/all_gather | solution.py:32
  9.9 6.8 %copy-start.14 = (bf16[128,8,128]{2,1,0:T(8,128)(2,1)}, bf16[128,8,128]{2,1,0:T(8,128)(2,1)S(1)}, u32[]{:S(2)}) copy-start(bf16[128,8,128]{2,1,0:T(8,128)(2,1)S(1)} %get-tuple-element.1834) | copy-start | bytes 786436
  10.0 10.4 %collective-permute-start = (bf16[128,8,128]{2,0,1:T(8,128)(2,1)S(1)}, bf16[128,8,128]{2,0,1:T(8,128)(2,1)S(1)}, u32[]{:S(2)}, u32[]{:S(2)}) collective-permute-start(bf16[128,8,128]{2,0,1:T(8,128)(2,1)S(1)} %copy.122), channel_id=1, source_target_pairs={{0,64},{64,0},{8,72},{72,8},{16,80},{80,16},{24,88},{88,24},{32,96... | collective-permute-start | bytes 786440 | tf_op jit(solution)/shard_map/ppermute | solution.py:19
  21.2 28.3 %copy-start.10 = (f32[128,8,128]{0,2,1:T(8,128)}, f32[128,8,128]{0,2,1:T(8,128)S(1)}, u32[]{:S(2)}) copy-start(f32[128,8,128]{0,2,1:T(8,128)S(1)} %get-tuple-element.1844) | copy-start | bytes 1572868
  129.8 6.1 %copy-start.1 = (bf16[128,8,256]{2,0,1:T(8,128)(2,1)}, bf16[128,8,256]{2,0,1:T(8,128)(2,1)S(1)}, u32[]{:S(2)}) copy-start(bf16[128,8,256]{2,0,1:T(8,128)(2,1)S(1)} %get-tuple-element.2367) | copy-start | bytes 1572868
  129.8 6.1 %copy-start.3 = (bf16[128,8,128]{2,0,1:T(8,128)(2,1)}, bf16[128,8,128]{2,0,1:T(8,128)(2,1)S(1)}, u32[]{:S(2)}) copy-start(bf16[128,8,128]{2,0,1:T(8,128)(2,1)S(1)} %get-tuple-element.2369) | copy-start | bytes 786436
  129.8 7.0 %copy-start.5 = (bf16[4096,128]{1,0:T(8,128)(2,1)}, bf16[4096,128]{1,0:T(8,128)(2,1)S(1)}, u32[]{:S(2)}) copy-start(bf16[4096,128]{1,0:T(8,128)(2,1)S(1)} %get-tuple-element.2370) | copy-start | bytes 3145732
  129.8 4.5 %copy-start.21 = (f32[128,8,128]{2,0,1:T(8,128)S(1)}, f32[128,8,128]{2,0,1:T(8,128)}, u32[]{:S(2)}) copy-start(f32[128,8,128]{2,0,1:T(8,128)} %get-tuple-element.1218) | copy-start | bytes 1572868
  129.8 4.5 %copy-start.30 = (f32[128,8]{0,1:T(8,128)S(1)}, f32[128,8]{0,1:T(8,128)}, u32[]{:S(2)}) copy-start(f32[128,8]{0,1:T(8,128)} %get-tuple-element.1221) | copy-start | bytes 12292
  150.0 3.2 copy-start.33
  165.2 3.2 copy-start.33
  180.4 3.2 copy-start.33
  195.6 3.2 copy-start.33
  210.8 3.2 copy-start.33
  223.1 3.2 copy-start.33
  235.4 3.2 copy-start.33
  247.7 3.2 copy-start.33
  252.8 1.3 copy-start.9
  252.8 1.3 copy-start.39
  252.8 1.3 copy-start.41
  254.1 3.0 copy-start.7
  254.2 3.0 copy-start.17
  254.2 3.0 copy-start.37
  254.2 3.0 copy-start.43
  255.8 2.9 copy-start.15
  257.2 1.5 copy-start.13
  257.2 1.7 copy-start.18
  258.9 1.5 copy-start.12
  260.3 1.4 copy-start.44
  260.3 72.5 %copy-start.35 = (f32[128,128]{1,0:T(8,128)S(1)}, f32[128,128]{1,0:T(8,128)}, u32[]{:S(2)}) copy-start(f32[128,128]{1,0:T(8,128)} %get-tuple-element.1228) | copy-start | bytes 196612
  (58 other events, 52.6 us)
Sparse Core Ops, SparseCore 0:
  10.3 36.5 all-gather.4
  261.9 81.3 all-gather.6
where the time goes:
time: 389 us; the launch traced here: 385 us
  blocking collectives  102 us (26%)
  matrix products  94.7 us (24%)
  local copies, waits for them, and re-layouts  73 us (19%)
  other arithmetic  42.7 us (11%)
  waiting for transfers between devices  25.9 us (7%)
  loops' own time  23.2 us (6%)
  between operations  19.4 us (5%)
  starting transfers between devices  4.15 us (1%)
    unnamed x1, blocking collectives  68.6 us
    dot_general x32, matrix products, listed_pairs(): jnp.dot(selector, pair_rows[number], precision=HIGHEST_PRECISION) > 0.5  30.5 us
    all_gather x1, waiting for transfers between devices, sent_together(): lax.all_gather(both, axis, axis=dim, tiled=True)  24.8 us
    while x48, local copies, waits for them, and re-layouts  22.2 us
    all_gather x1, blocking collectives, total_of_pieces(): tiles = lax.all_gather(shard, axis).astype(jnp.float32)  19.3 us
    all_to_all x1, blocking collectives, sent_to_all(): return lax.all_to_all(copies, axis, split_axis=0, concat_axis=0, tiled=True)  14.1 us
    reduce_or x8, other arithmetic, backward_turn(): jnp.any(allowed)  11.8 us
    another operation x1, loops' own time, body(): lax.fori_loop(0, row_count // backward_slab_rows, backward_turn, (empty_g...  11.1 us
  transfers between devices with their start and end apart: 3, of which 2 were waited for; matrix products, arithmetic and copies ran while one was open for 2% of the time, Pallas kernels for 0%

commit v1 on v0

v1 whole, which is shorter than its diff:
```python
import math

import jax
import jax.numpy as jnp
from jax import lax
from jax.experimental import pallas as pl
from jax.experimental.pallas import tpu as pltpu
from jax.sharding import PartitionSpec as P


BLK = 128
HD = 128
HEADS = 8
SEQ = 16
KV = 8
SLOTS = 18
STEPS = SLOTS // 2
FLOOR = -1e30
LOG2E = 1.4426950408889634
ROWS = 72
PAYLOAD = 80
BF16 = jnp.bfloat16
F32 = jnp.float32

SAME_CORE = [[core + 2 * chip for chip in range(SEQ // 2)] for core in range(2)]
OTHER_CORE = [(i, i ^ 1) for i in range(SEQ)]
MIRROR = [(i, SEQ - 1 - i) for i in range(SEQ)]


def dot(a, b):
    return jnp.dot(a, b, preferred_element_type=F32)


def dot_nt(a, b):
    return lax.dot_general(a, b, (((1,), (1,)), ((), ())), preferred_element_type=F32)


def split_bf16(x):
    high = x.astype(BF16)
    return high, (x - high.astype(F32)).astype(BF16)


def halves(u, axis):
    top = jnp.max(u, axis=axis, keepdims=True)
    low = jnp.min(u, axis=axis, keepdims=True)
    up = jnp.exp(u - top)
    down = jnp.exp(low - u)
    up = up / jnp.sum(up, axis=axis, keepdims=True)
    down = down / jnp.sum(down, axis=axis, keepdims=True)
    return up, down


def list_blocks(mine, pairs, info):
    late = 2 * (SEQ - 1 - mine) + 1
    odd = lax.rem(mine, 2)
    for slot in range(SLOTS):
        info[slot] = 0
    info[0] = 2 * mine
    info[2] = late
    late_first = 4 + 2 * (mine // 2)

    def scan(row, counts):
        early_count, late_count = counts
        query = pairs[2 * row]
        key = pairs[2 * row + 1]
        earlier = query != key
        is_early = (query == 2 * mine) & earlier
        is_late = (query == late) & earlier

        @pl.when(is_early | is_late)
        def _():
            early_slot = jnp.where(early_count < odd, 1, 4 + early_count - odd)
            late_slot = jnp.where(late_count < 1 - odd, 3, late_first + late_count - (1 - odd))
            info[jnp.minimum(jnp.where(is_early, early_slot, late_slot), SLOTS - 1)] = key

        return (
            early_count + jnp.where(is_early, 1, 0),
            late_count + jnp.where(is_late, 1, 0),
        )

    lax.fori_loop(0, pairs.shape[0] // 2, scan, (jnp.int32(0), jnp.int32(0)))
    info[32] = jnp.where(odd == 1, 2 * BLK, -2 * BLK)
    info[33] = jnp.where(odd == 1, -2 * BLK, 2 * BLK)
    info[34] = 2 + mine // 2
    info[35] = odd


def features(q, q_map_t, q_t, mapped_t, mapped, soft_t):
    for head in range(HEADS):
        lanes = pl.ds(head * BLK, BLK)
        rows_t = q[head].T
        q_t[:, lanes] = rows_t
        up, down = halves(dot(q_map_t[head], rows_t), 0)
        soft = jnp.concatenate([up, down], axis=0)
        soft_t[:, lanes] = soft
        mapped_t[:, lanes] = soft.astype(BF16)
        mapped[lanes, :] = soft.T.astype(BF16)


def early_kernel(place, pairs, q, q_map_t, q_t, mapped_t, mapped, soft_t, info):
    list_blocks(place[0], pairs, info)
    features(q, q_map_t, q_t, mapped_t, mapped, soft_t)


def late_kernel(q, q_map_t, q_t, mapped_t, mapped, soft_t):
    features(q, q_map_t, q_t, mapped_t, mapped, soft_t)


def main_kernel(
    info, same, other, k_map,
    q_t0, mapped_t0, mapped0, soft_t0, q_t1, mapped_t1, mapped1, soft_t1,
    out,
    q_t, mapped_t, mapped, soft_t, kv, kv_sems, q_sems, v_t, k_t, soft_k, mk, mk_t,
    t_acc, s_acc, m_acc, l_acc, n_acc, gn, gnorm, gqf, gk_acc, flat, loss_acc,
    s_buf, p_buf, x_buf, kf_buf,
):
    parity = info[35]
    switch = info[34]

    def start_slot(slot):
        block = info[slot]
        chip = block // 4
        first = pl.multiple_of(lax.rem(block, 2) * BLK, BLK)
        near = lax.rem(block // 2, 2) == parity

        @pl.when(near)
        def _():
            pltpu.make_async_copy(
                same.at[chip, pl.ds(first, BLK)], kv.at[slot], kv_sems.at[slot]
            ).start()

        @pl.when(jnp.logical_not(near))
        def _():
            pltpu.make_async_copy(
                other.at[chip, pl.ds(first, BLK)], kv.at[slot], kv_sems.at[slot]
            ).start()

    def wait_slot(slot):
        pltpu.make_async_copy(same.at[0, pl.ds(0, BLK)], kv.at[slot], kv_sems.at[slot]).wait()

    loads = []
    for side, refs in enumerate(((q_t0, mapped_t0, mapped0, soft_t0), (q_t1, mapped_t1, mapped1, soft_t1))):
        for number, (ref, held) in enumerate(zip(refs, (q_t, mapped_t, mapped, soft_t))):
            loads.append(pltpu.make_async_copy(ref, held.at[side], q_sems.at[side, number]))
    for slot in range(4):
        start_slot(slot)
    loads[0].start()
    loads[1].start()
    loads[4].start()
    loads[5].start()
    for slot in range(4, SLOTS):
        start_slot(slot)
    for number in (2, 6, 3, 7):
        loads[number].start()

    def key_rows(step):
        return jnp.concatenate([kv[2 * step, :, :HD], kv[2 * step + 1, :, :HD]], axis=0)

    def value_rows(step):
        return jnp.concatenate([kv[2 * step, :, HD:], kv[2 * step + 1, :, HD:]], axis=0)

    def prepare(step):
        keys = key_rows(step)
        up, down = halves(dot(keys, k_map[...]), 1)
        soft = jnp.concatenate([up, down], axis=1)
        soft_k[step] = soft
        mk[step] = soft.astype(BF16)
        mk_t[step] = soft.T.astype(BF16)
        v_t[step] = value_rows(step).T
        k_t[step] = keys.T

    def allowed_of(side):
        key_minus_query = lax.broadcasted_iota(jnp.int32, (BLK, BLK), 0) - (
            lax.broadcasted_iota(jnp.int32, (BLK, BLK), 1)
        )
        tall = jnp.concatenate(
            [key_minus_query <= 0, key_minus_query <= info[32 + side]], axis=0
        )
        return jnp.concatenate([tall, tall], axis=1)

    shrink = LOG2E / math.sqrt(HD)
    wide = 2 * BLK
    chunks = HEADS // 2

    def forward(step, side, first):
        allowed = allowed_of(side) if first else None
        keys = key_rows(step)
        for c in range(chunks):
            lanes = pl.ds(c * wide, wide)
            scores = dot(keys, q_t[side, :, lanes])
            if first:
                scores = jnp.where(allowed, scores, FLOOR)
            s_buf[:, lanes] = scores
            new = jnp.max(scores, axis=0, keepdims=True)
            if first:
                m_acc[side, c] = new
            else:
                old = m_acc[side, c]
                new = jnp.maximum(old, new)
                m_acc[side, c] = new
                shift = jnp.exp2((old - new) * shrink)
                l_acc[side, c] = l_acc[side, c] * shift
                t_acc[side, c] = t_acc[side, c] * shift
        for c in range(chunks):
            lanes = pl.ds(c * wide, wide)
            mixing = dot(mk[step], mapped_t[side, :, lanes])
            if first:
                mixing = jnp.where(allowed, mixing, 0.0)
            total = jnp.sum(mixing, axis=0, keepdims=True)
            n_acc[side, c] = total if first else n_acc[side, c] + total
            x_buf[:, lanes] = mixing.astype(BF16)
        for c in range(chunks):
            lanes = pl.ds(c * wide, wide)
            weights = jnp.exp2((s_buf[:, lanes] - m_acc[side, c]) * shrink)
            total = jnp.sum(weights, axis=0, keepdims=True)
            l_acc[side, c] = total if first else l_acc[side, c] + total
            p_buf[:, lanes] = weights.astype(BF16)
        for c in range(chunks):
            lanes = pl.ds(c * wide, wide)
            product = dot(v_t[step], x_buf[:, lanes])
            s_acc[side, c] = product if first else s_acc[side, c] + product
        for c in range(chunks):
            lanes = pl.ds(c * wide, wide)
            product = dot(v_t[step], p_buf[:, lanes])
            t_acc[side, c] = product if first else t_acc[side, c] + product

    def wait_step(step):
        wait_slot(2 * step)
        wait_slot(2 * step + 1)

    def side_of(step):
        return jnp.where(step >= switch, 1, 0)

    wait_step(0)
    prepare(0)
    loads[0].wait()
    loads[1].wait()
    forward(0, 0, True)
    wait_step(1)
    prepare(1)
    loads[4].wait()
    loads[5].wait()
    wait_step(2)
    forward(1, 1, True)
    prepare(2)

    def forward_turn(step, carry):
        later = jnp.minimum(step + 1, STEPS - 1)

        @pl.when(step < STEPS - 1)
        def _():
            wait_step(later)

        forward(step, side_of(step), False)
        prepare(later)
        return carry

    lax.fori_loop(2, STEPS, forward_turn, 0)

    def settle(side, loss):
        for c in range(chunks):
            norm = 1.0 / n_acc[side, c]
            student = s_acc[side, c] * norm
            mismatch = student - t_acc[side, c] * (1.0 / l_acc[side, c])
            upstream = 2.0 * mismatch
            gn[side, c] = (upstream * norm).astype(BF16)
            gnorm[side, c] = -jnp.sum(upstream * student, axis=0, keepdims=True) * norm
            loss = loss + jnp.sum(mismatch * mismatch, axis=0, keepdims=True)
        return loss

    loss = lax.fori_loop(0, 2, settle, jnp.zeros((1, wide), F32))
    loss_acc[...] = jnp.broadcast_to(loss[:, :BLK] + loss[:, BLK:], loss_acc.shape)

    def key_back(step):
        grad_kf = kf_buf[...]
        soft = soft_k[step]
        lead, trail = soft[:, :HD], soft[:, HD:]
        g_lead, g_trail = grad_kf[:, :HD], grad_kf[:, HD:]
        back = lead * (g_lead - jnp.sum(lead * g_lead, axis=1, keepdims=True)) - trail * (
            g_trail - jnp.sum(trail * g_trail, axis=1, keepdims=True)
        )
        high, low = split_bf16(back)
        return dot(k_t[step], high) + dot(k_t[step], low)

    def backward(step, side, first):
        allowed = allowed_of(side) if first else None
        values = value_rows(step)
        for c in range(chunks):
            lanes = pl.ds(c * wide, wide)
            grad = dot(values, gn[side, c]) + gnorm[side, c]
            if first:
                grad = jnp.where(allowed, grad, 0.0)
            p_buf[:, lanes] = grad.astype(BF16)
        for c in range(chunks):
            lanes = pl.ds(c * wide, wide)
            product = dot(mk_t[step], p_buf[:, lanes])
            gqf[side, c] = product if first else gqf[side, c] + product
        kf_buf[...] = dot(p_buf[...], mapped[side])

    loads[2].wait()
    backward(0, 0, True)
    gk_acc[...] = key_back(0)
    loads[6].wait()
    backward(1, 1, True)

    def backward_turn(step, carry):
        gk_acc[...] = gk_acc[...] + key_back(step - 1)
        backward(step, side_of(step), False)
        return carry

    lax.fori_loop(2, STEPS, backward_turn, 0)
    loads[3].wait()
    loads[7].wait()
    flat[pl.ds(HEADS * HD, HD)] = gk_acc[...] + key_back(STEPS - 1)

    for head in range(HEADS):
        total = jnp.zeros((HD, HD), F32)
        lanes = pl.ds(head * BLK, BLK)
        column = (head % 2) * BLK
        for side in range(2):
            lead, trail = soft_t[side, :HD, lanes], soft_t[side, HD:, lanes]
            g_lead = gqf[side, head // 2, :HD, pl.ds(column, BLK)]
            g_trail = gqf[side, head // 2, HD:, pl.ds(column, BLK)]
            back = lead * (g_lead - jnp.sum(lead * g_lead, axis=0, keepdims=True)) - trail * (
                g_trail - jnp.sum(trail * g_trail, axis=0, keepdims=True)
            )
            high, low = split_bf16(back)
            rows_t = q_t[side, :, lanes]
            total = total + dot_nt(rows_t, high) + dot_nt(rows_t, low)
        flat[pl.ds(head * HD, HD)] = total
    high, low = split_bf16(loss_acc[...])
    tail = jnp.concatenate([high[:1], low[:1], jnp.zeros((6, BLK), BF16)], axis=0)
    for piece in range(SEQ):
        out[piece, pl.ds(0, ROWS)] = flat[pl.ds(piece * ROWS, ROWS)].astype(BF16)
        out[piece, pl.ds(ROWS, PAYLOAD - ROWS)] = tail


def fold_kernel(pieces, chunk, stats):
    total = jnp.sum(pieces[...].astype(F32), axis=0)
    grads = total[:ROWS]
    chunk[...] = grads.astype(BF16)
    squares = jnp.sum(grads * grads, axis=0, keepdims=True)
    loss = total[ROWS : ROWS + 1] + total[ROWS + 1 : ROWS + 2]
    rows = jnp.concatenate([squares, loss, jnp.zeros((6, BLK), F32)], axis=0)
    for peer in range(KV):
        stats[peer] = rows


def share_kernel(chunk, stats, payload, loss):
    total = jnp.sum(stats[...], axis=0)
    high, low = split_bf16(total)
    tail = jnp.concatenate([high[:1], low[:1], jnp.zeros((6, BLK), BF16)], axis=0)
    for peer in range(SEQ):
        payload[peer, pl.ds(0, ROWS)] = chunk[...]
        payload[peer, pl.ds(ROWS, PAYLOAD - ROWS)] = tail
    loss[...] = jnp.broadcast_to(
        jnp.sum(total[1:2], axis=1, keepdims=True) / (SEQ * 2 * BLK * KV * HEADS * HD), loss.shape
    )


def scale_kernel(pieces, q_out, k_out):
    tail = pieces[:, ROWS:, :].astype(F32)
    squared = jnp.sum(tail[:, 0, :] + tail[:, 1, :], axis=0, keepdims=True)
    squared = jnp.sum(squared, axis=1, keepdims=True)
    scale = jnp.sqrt(squared / ((HEADS + 1) * KV * HD * HD) + 1e-06)
    heads = HEADS * HD
    for piece in range(SEQ):
        rows = pieces[piece, pl.ds(0, ROWS)].astype(F32) / scale
        first = piece * ROWS
        keep = min(max(heads - first, 0), ROWS)
        if keep:
            q_out[pl.ds(first, keep)] = rows[:keep]
        if keep < ROWS:
            k_out[pl.ds(first + keep - heads, ROWS - keep)] = rows[keep:]


def vmem():
    return pl.BlockSpec(memory_space=pltpu.VMEM)


def smem():
    return pl.BlockSpec(memory_space=pltpu.SMEM)


def shape(dims, kind):
    return jax.ShapeDtypeStruct(dims, kind)


def any_space():
    return pl.BlockSpec(memory_space=pl.ANY)


def feature_shapes():
    wide = HEADS * BLK
    return (
        shape((HD, wide), BF16),
        shape((2 * HD, wide), BF16),
        shape((wide, 2 * HD), BF16),
        shape((2 * HD, wide), F32),
    )


def layer(queries, keys, values, q_map, k_map, block_pairs):
    place = lax.axis_index("seq").astype(jnp.int32).reshape(1)
    late = lax.ppermute(queries[BLK:], "seq", MIRROR)
    many = (SEQ // 2, 2 * BLK, HD)
    sent = jnp.concatenate(
        [jnp.broadcast_to(keys[:, 0, :], many), jnp.broadcast_to(values[:, 0, :], many)], axis=2
    )
    same = lax.all_to_all(sent, "seq", 0, 0, axis_index_groups=SAME_CORE, tiled=True)
    other = lax.ppermute(same, "seq", OTHER_CORE)

    cost = pl.CostEstimate(flops=5 * 10**9, bytes_accessed=10**7, transcendentals=10**6)
    q_map_t = jnp.transpose(q_map, (0, 2, 1))
    *early_parts, info = pl.pallas_call(
        early_kernel,
        out_shape=(*feature_shapes(), shape((128,), jnp.int32)),
        in_specs=[smem(), smem(), vmem(), vmem()],
        out_specs=(vmem(), vmem(), vmem(), vmem(), smem()),
        cost_estimate=cost,
        name="early_features",
    )(place, block_pairs.reshape(-1), jnp.transpose(queries[:BLK], (1, 0, 2)), q_map_t)
    late_parts = pl.pallas_call(
        late_kernel,
        out_shape=feature_shapes(),
        in_specs=[vmem(), vmem()],
        out_specs=(vmem(), vmem(), vmem(), vmem()),
        cost_estimate=cost,
        name="late_features",
    )(jnp.transpose(late, (1, 0, 2)), q_map_t)

    wide = HEADS * BLK
    pair = 2 * BLK
    chunks = HEADS // 2
    out = pl.pallas_call(
        main_kernel,
        out_shape=shape((SEQ, PAYLOAD, BLK), BF16),
        in_specs=[smem(), any_space(), any_space(), vmem()] + [any_space()] * 8,
        out_specs=vmem(),
        scratch_shapes=[
            pltpu.VMEM((2, HD, wide), BF16),
            pltpu.VMEM((2, 2 * HD, wide), BF16),
            pltpu.VMEM((2, wide, 2 * HD), BF16),
            pltpu.VMEM((2, 2 * HD, wide), F32),
            pltpu.VMEM((SLOTS, BLK, 2 * HD), BF16),
            pltpu.SemaphoreType.DMA((SLOTS,)),
            pltpu.SemaphoreType.DMA((2, 4)),
            pltpu.VMEM((STEPS, HD, pair), BF16),
            pltpu.VMEM((STEPS, HD, pair), BF16),
            pltpu.VMEM((STEPS, pair, 2 * HD), F32),
            pltpu.VMEM((STEPS, pair, 2 * HD), BF16),
            pltpu.VMEM((STEPS, 2 * HD, pair), BF16),
            pltpu.VMEM((2, chunks, HD, pair), F32),
            pltpu.VMEM((2, chunks, HD, pair), F32),
            pltpu.VMEM((2, chunks, 1, pair), F32),
            pltpu.VMEM((2, chunks, 1, pair), F32),
            pltpu.VMEM((2, chunks, 1, pair), F32),
            pltpu.VMEM((2, chunks, HD, pair), BF16),
            pltpu.VMEM((2, chunks, 1, pair), F32),
            pltpu.VMEM((2, chunks, 2 * HD, pair), F32),
            pltpu.VMEM((HD, HD), F32),
            pltpu.VMEM(((HEADS + 1) * HD, HD), F32),
            pltpu.VMEM((8, BLK), F32),
            pltpu.VMEM((pair, wide), F32),
            pltpu.VMEM((pair, wide), BF16),
            pltpu.VMEM((pair, wide), BF16),
            pltpu.VMEM((pair, 2 * HD), F32),
        ],
        compiler_params=pltpu.CompilerParams(vmem_limit_bytes=56 * 1024 * 1024),
        name="attend",
    )(info, same, other, k_map[0], *early_parts, *late_parts)

    pieces = lax.all_to_all(out, "seq", 0, 0, tiled=True)
    chunk, stats = pl.pallas_call(
        fold_kernel,
        out_shape=(shape((ROWS, BLK), BF16), shape((KV, 8, BLK), F32)),
        in_specs=[vmem()],
        out_specs=(vmem(), vmem()),
        name="fold",
    )(pieces)
    stats = lax.all_to_all(stats, "kv", 0, 0, tiled=True)
    payload, loss = pl.pallas_call(
        share_kernel,
        out_shape=(shape((SEQ, PAYLOAD, BLK), BF16), shape((8, BLK), F32)),
        in_specs=[vmem(), vmem()],
        out_specs=(vmem(), vmem()),
        name="share",
    )(chunk, stats)
    shared = lax.all_to_all(payload, "seq", 0, 0, tiled=True)
    grad_q, grad_k = pl.pallas_call(
        scale_kernel,
        out_shape=(shape((HEADS * HD, HD), F32), shape((HD, HD), F32)),
        in_specs=[vmem()],
        out_specs=(vmem(), vmem()),
        name="scale",
    )(shared)
    return grad_q.reshape(HEADS, HD, HD), grad_k.reshape(1, HD, HD), loss[0, 0]


def solution(mesh):
    placed = (
        P("seq", "kv", None),
        P("seq", "kv", None),
        P("seq", "kv", None),
        P("kv", None, None),
        P("kv", None, None),
        P(),
    )
    return jax.shard_map(
        layer,
        mesh=mesh,
        in_specs=placed,
        out_specs=(P("kv", None, None), P("kv", None, None), P()),
        check_vma=False,
    )
```

time: 389 us -> 111 us (0.29)
  matrix products: 94.7 us -> 0 us
  local copies, waits for them, and re-layouts: 73 us -> 8.04 us
  blocking collectives: 102 us -> 49.7 us
  other arithmetic: 42.7 us -> 0.12 us
  Pallas kernels: 0 us -> 38.4 us
  loops' own time: 23.2 us -> 0 us
  between operations: 19.4 us -> 0.74 us
  waiting for transfers between devices: 25.9 us -> 7.49 us
    dot_general x103 -> x0, matrix products: 93.1 us -> none  [the longest x32 30.5 us: listed_pairs(): jnp.dot(selector, pair_rows[number], precision=HIGHEST_PRECISION) > 0.5]
    unnamed x1 -> x0, blocking collectives: 68.6 us -> none
    pallas_call x0 -> x6, Pallas kernels: none -> 38.4 us  [the longest x1 24 us: layer(): pl.pallas_call(main_kernel, out_shape=shape((SEQ, PAYLOAD, BLK), BF16), i...]
    all_to_all x1 -> x3, blocking collectives: 14.1 us -> 49.7 us  [the longest x1 22.2 us: layer(): lax.all_to_all(sent, 'seq', 0, 0, axis_index_groups=SAME_CORE, tiled=True)]
    while x50 -> x0, local copies, waits for them, and re-layouts: 24.9 us -> none
    all_gather x2 -> x0, waiting for transfers between devices: 24.8 us -> none  [the longest x1 24.8 us: sent_together(): lax.all_gather(both, axis, axis=dim, tiled=True)]
    another operation x34 -> x0, loops' own time: 23.2 us -> none  [the longest x1 11.1 us: body(): lax.fori_loop(0, row_count // backward_slab_rows, backward_turn, (empty_g...]
    all_gather x1 -> x0, blocking collectives: 19.3 us -> none  [total_of_pieces(): tiles = lax.all_gather(shard, axis).astype(jnp.float32)]
  transfers between devices with their start and end apart: 3 -> 3, of which waited for: 2 -> 1; matrix products, arithmetic and copies ran while one was open for 2% -> 3% of each run, Pallas kernels for 0% -> 8%
where the time goes in v1:
time: 111 us; the launch traced here: 110 us
  blocking collectives  49.7 us (45%)
  Pallas kernels  38.4 us (35%)
  local copies, waits for them, and re-layouts  8.04 us (7%)
  waiting for transfers between devices  7.49 us (7%)
  starting transfers between devices  5.21 us (5%)
    pallas_call x1, Pallas kernels, layer(): pl.pallas_call(main_kernel, out_shape=shape((SEQ, PAYLOAD, BLK), BF16), i...  24 us
    all_to_all x1, blocking collectives, layer(): lax.all_to_all(sent, 'seq', 0, 0, axis_index_groups=SAME_CORE, tiled=True)  22.2 us
    all_to_all x1, blocking collectives, layer(): stats = lax.all_to_all(stats, 'kv', 0, 0, tiled=True)  14.5 us
    all_to_all x1, blocking collectives, layer(): pieces = lax.all_to_all(out, 'seq', 0, 0, tiled=True)  12.9 us
    all_to_all x1, waiting for transfers between devices, layer(): shared = lax.all_to_all(payload, 'seq', 0, 0, tiled=True)  7.49 us
    pallas_call x1, Pallas kernels, layer(): pl.pallas_call(early_kernel, out_shape=(*feature_shapes(), shape((128,),...  6.25 us
    unnamed x18, local copies, waits for them, and re-layouts  4.25 us
    all_to_all x1, starting transfers between devices, layer(): shared = lax.all_to_all(payload, 'seq', 0, 0, tiled=True)  3.54 us
  transfers between devices with their start and end apart: 3, of which 1 were waited for; matrix products, arithmetic and copies ran while one was open for 3% of the time, Pallas kernels for 8%

profile of v1, /device:TPU:0, one launch (start us, length us, event | category | flops | bytes accessed | tf_op | source)
XLA Modules:
  0.0 109.6 jit_solution(1731245393819621260)
XLA Ops:
  0.6 0.9 broadcast_in_dim.6
  1.5 0.9 broadcast_in_dim.7
  2.5 0.1 pad_maximum_fusion
  2.6 0.0 copy-start.3
  2.6 22.2 %all_to_all.20.same = bf16[8,256,256]{2,1,0:T(8,128)(2,1)S(1)} all-to-all(bf16[8,256,256]{2,1,0:T(8,128)(2,1)S(1)} %pad_maximum_fusion), channel_id=1, replica_groups={{0,16,32,48,64,80,96,112},{8,24,40,56,72,88,104,120},{1,17,33,49,65,81,..., dimensions={0} | all-to-all | bytes 2097152 | tf_op jit(solution)/shard_map/all_to_all | solution.py:410
  24.8 0.0 collective-permute-start
  24.8 0.0 copy-done.3
  24.9 0.0 copy-start.5
  24.9 1.7 %collective-permute-start.1 = (bf16[128,8,128]{2,0,1:T(8,128)(2,1)S(1)}, bf16[128,8,128]{2,0,1:T(8,128)(2,1)S(1)}, u32[]{:S(2)}, u32[]{:S(2)}) collective-permute-start(bf16[128,8,128]{2,0,1:T(8,128)(2,1)S(1)} %copy.17), channel_id=1, source_target_pairs={{0,120},{8,112},{16,104},{24,96},{32,88},{40,80},{48,72},{56,64},{... | collective-permute-start | bytes 786440 | tf_op jit(solution)/shard_map/ppermute | solution.py:405
  26.6 0.8 copy.19
  27.3 0.0 copy-done
  27.3 0.0 copy-done.4
  27.3 0.9 copy.14
  28.2 0.0 copy-done.5
  28.2 0.1 copy.12
  28.4 0.7 reshape.19.pairs
  29.1 6.3 %early_features.1 = (bf16[128,1024]{1,0:T(8,128)(2,1)}, bf16[256,1024]{1,0:T(8,128)(2,1)}, bf16[1024,256]{1,0:T(8,128)(2,1)}, f32[256,1024]{1,0:T(8,128)}, s32[128]{0:T(128)}) custom-call(s32[1]{0:T(128)} %bitcast.place, s32[544]{0:T(1024)} %reshape.19.pairs, bf16[8,128,128]{2,1,0:T(8,128)(2,1)} %bitcast.14, bf16[8,128,128]{2,1,0:T(8,128)(2,1)} %bitcast.12), custom_call_target="tpu_custom_call" | custom-call | flops 5000000000 | bytes 10000000 | tf_op jit(solution)/shard_map/early_features/pallas_call | solution.py:415
  35.4 0.0 collective-permute-done.1
  35.4 0.7 copy-done.6
  36.1 3.0 %late_features.1 = (bf16[128,1024]{1,0:T(8,128)(2,1)}, bf16[256,1024]{1,0:T(8,128)(2,1)}, bf16[1024,256]{1,0:T(8,128)(2,1)}, f32[256,1024]{1,0:T(8,128)}) custom-call(bf16[8,128,128]{2,1,0:T(8,128)(2,1)} %bitcast.19, bf16[8,128,128]{2,1,0:T(8,128)(2,1)} %bitcast.13), custom_call_target="tpu_custom_call" | custom-call | flops 5000000000 | bytes 10000000 | tf_op jit(solution)/shard_map/late_features/pallas_call | solution.py:423
  39.1 0.0 collective-permute-done.other
  39.1 1.0 copy-done.2
  40.1 24.0 %attend.1 = bf16[16,80,128]{2,1,0:T(8,128)(2,1)} custom-call(s32[128]{0:T(128)} %get-tuple-element.18.info, bf16[8,256,256]{2,1,0:T(8,128)(2,1)} %copy-done, bf16[8,256,256]{2,1,0:T(8,128)(2,1)} %copy-done.2, bf16[128,128]{1,0:T(8,128)(2,1)} %bitcast.17, bf16[128,1024]{1,0:T(8,128)(2,1)} %get-tuple-element.19.q_t0, ...), custom_call_target="tpu_custom_call" | custom-call | tf_op jit(solution)/shard_map/attend/pallas_call | solution.py:435
  64.1 12.9 %all_to_all.21.pieces = bf16[16,80,128]{2,1,0:T(8,128)(2,1)} all-to-all(bf16[16,80,128]{2,1,0:T(8,128)(2,1)} %attend.1), channel_id=1, replica_groups=mesh['seq'=16,'kv'=8] {'seq'}, dimensions={0} | all-to-all | bytes 655360 | tf_op jit(solution)/shard_map/all_to_all | solution.py:473
  77.0 1.6 %fold.1 = (bf16[72,128]{1,0:T(8,128)(2,1)}, f32[8,8,128]{2,1,0:T(8,128)}) custom-call(bf16[16,80,128]{2,1,0:T(8,128)(2,1)} %all_to_all.21.pieces), custom_call_target="tpu_custom_call" | custom-call | tf_op jit(solution)/shard_map/fold/pallas_call | solution.py:474
  78.7 14.5 %all_to_all.22.stats = f32[8,8,128]{2,1,0:T(8,128)} all-to-all(f32[8,8,128]{2,1,0:T(8,128)} %get-tuple-element.28), channel_id=1, replica_groups=mesh['seq'=16,'kv'=8] {'kv'}, dimensions={0} | all-to-all | bytes 65536 | tf_op jit(solution)/shard_map/all_to_all | solution.py:481
  93.2 1.5 %share.1 = (bf16[16,80,128]{2,1,0:T(8,128)(2,1)}, f32[8,128]{1,0:T(8,128)}) custom-call(bf16[72,128]{1,0:T(8,128)(2,1)} %get-tuple-element.27.chunk, f32[8,8,128]{2,1,0:T(8,128)} %all_to_all.22.stats), custom_call_target="tpu_custom_call" | custom-call | tf_op jit(solution)/shard_map/share/pallas_call | solution.py:482
  94.8 3.5 %all-to-all-start.3 = ((bf16[16,80,128]{2,1,0:T(8,128)(2,1)}), bf16[16,80,128]{2,1,0:T(8,128)(2,1)S(1)}, u32[]{:S(2)}, u32[]{:S(2)}) async-start(bf16[16,80,128]{2,1,0:T(8,128)(2,1)} %get-tuple-element.29), calls=%async_computation.3 | async-start | bytes 655360 | tf_op jit(solution)/shard_map/all_to_all | solution.py:489
  98.3 1.2 %slice.11 = f32[1,1]{1,0:T(1,128)} slice(f32[8,128]{1,0:T(8,128)} %get-tuple-element.32), slice={[0:1], [0:1]} | slice | bytes 8 | tf_op jit(solution)/shard_map/slice | solution.py:497
  99.5 7.5 %all-to-all-done.3.pieces = bf16[16,80,128]{2,1,0:T(8,128)(2,1)S(1)} async-done(((bf16[16,80,128]{2,1,0:T(8,128)(2,1)}), bf16[16,80,128]{2,1,0:T(8,128)(2,1)S(1)}, u32[]{:S(2)}, u32[]{:S(2)}) %all-to-all-start.3) | async-done | bytes 327712 | tf_op jit(solution)/shard_map/all_to_all | solution.py:489
  107.0 0.7 copy-done.1
  107.7 1.9 %scale.1 = (f32[1024,128]{1,0:T(8,128)}, f32[128,128]{1,0:T(8,128)}) custom-call(bf16[16,80,128]{2,1,0:T(8,128)(2,1)} %copy-done.1), custom_call_target="tpu_custom_call" | custom-call | tf_op jit(solution)/shard_map/scale/pallas_call | solution.py:490
  (7 shorter events, 0.1 us)
Async XLA Ops:
  2.6 22.2 %copy-start.3 = (bf16[256,8,128]{2,1,0:T(8,128)(2,1)S(1)}, bf16[256,8,128]{2,1,0:T(8,128)(2,1)}, u32[]{:S(2)}) copy-start(bf16[256,8,128]{2,1,0:T(8,128)(2,1)} %param.6) | copy-start | bytes 1572868
  24.8 2.5 %copy-start = (bf16[8,256,256]{2,1,0:T(8,128)(2,1)}, bf16[8,256,256]{2,1,0:T(8,128)(2,1)S(1)}, u32[]{:S(2)}) copy-start(bf16[8,256,256]{2,1,0:T(8,128)(2,1)S(1)} %all_to_all.20.same) | copy-start | bytes 3145732
  24.8 2.5 %copy-start.4 = (bf16[8,128,128]{2,1,0:T(8,128)(2,1)S(1)}, bf16[8,128,128]{2,1,0:T(8,128)(2,1)}, u32[]{:S(2)}) copy-start(bf16[8,128,128]{2,1,0:T(8,128)(2,1)} %param.9) | copy-start | bytes 786436
  24.8 14.3 %collective-permute-start = (bf16[8,256,256]{2,1,0:T(8,128)(2,1)S(1)}, bf16[8,256,256]{2,1,0:T(8,128)(2,1)S(1)}, u32[]{:S(2)}, u32[]{:S(2)}) collective-permute-start(bf16[8,256,256]{2,1,0:T(8,128)(2,1)S(1)} %all_to_all.20.same), channel_id=1, source_target_pairs={{0,8},{8,0},{16,24},{24,16},{32,40},{40,32},{48,56},{56,48},{64,72... | collective-permute-start | bytes 3145736 | tf_op jit(solution)/shard_map/ppermute | solution.py:411
  24.9 3.4 %copy-start.5 = (s32[272,2]{0,1:T(2,128)S(1)}, s32[272,2]{0,1:T(2,128)}, u32[]{:S(2)}) copy-start(s32[272,2]{0,1:T(2,128)} %param.11) | copy-start | bytes 6532
  24.9 10.4 %collective-permute-start.1 = (bf16[128,8,128]{2,0,1:T(8,128)(2,1)S(1)}, bf16[128,8,128]{2,0,1:T(8,128)(2,1)S(1)}, u32[]{:S(2)}, u32[]{:S(2)}) collective-permute-start(bf16[128,8,128]{2,0,1:T(8,128)(2,1)S(1)} %copy.17), channel_id=1, source_target_pairs={{0,120},{8,112},{16,104},{24,96},{32,88},{40,80},{48,72},{56,64},{... | collective-permute-start | bytes 786440 | tf_op jit(solution)/shard_map/ppermute | solution.py:405
  35.4 0.7 copy-start.6
  39.1 1.0 copy-start.2
  94.8 12.2 %all-to-all-start.3 = ((bf16[16,80,128]{2,1,0:T(8,128)(2,1)}), bf16[16,80,128]{2,1,0:T(8,128)(2,1)S(1)}, u32[]{:S(2)}, u32[]{:S(2)}) async-start(bf16[16,80,128]{2,1,0:T(8,128)(2,1)} %get-tuple-element.29), calls=%async_computation.3 | async-start | bytes 655360 | tf_op jit(solution)/shard_map/all_to_all | solution.py:489
  107.0 0.7 copy-start.1

commit v2 on v1

v2 whole, which is shorter than its diff:
```python
import math

import jax
import jax.numpy as jnp
from jax import lax
from jax.experimental import pallas as pl
from jax.experimental.pallas import tpu as pltpu
from jax.sharding import PartitionSpec as P


BLK = 128
HD = 128
HEADS = 8
SEQ = 16
KV = 8
CHIPS = SEQ // 2
SLOTS = 18
STEPS = SLOTS // 2
UNROLL = 7
ATTEND_VMEM = 26 * 1024 * 1024
SMALL_VMEM = 4 * 1024 * 1024
FLOOR = -1e30
LOG2E = 1.4426950408889634
ROWS = 72
PAYLOAD = 80
BF16 = jnp.bfloat16
F32 = jnp.float32

SAME_CORE = [[core + 2 * chip for chip in range(SEQ // 2)] for core in range(2)]
OTHER_CORE = [(i, i ^ 1) for i in range(SEQ)]
MIRROR = [(i, SEQ - 1 - i) for i in range(SEQ)]


def dot(a, b):
    return jnp.dot(a, b, preferred_element_type=F32)


def dot_nt(a, b):
    return lax.dot_general(a, b, (((1,), (1,)), ((), ())), preferred_element_type=F32)


def split_bf16(x):
    high = x.astype(BF16)
    return high, (x - high.astype(F32)).astype(BF16)


def halves(u, axis):
    top = jnp.max(u, axis=axis, keepdims=True)
    low = jnp.min(u, axis=axis, keepdims=True)
    up = jnp.exp(u - top)
    down = jnp.exp(low - u)
    up = up / jnp.sum(up, axis=axis, keepdims=True)
    down = down / jnp.sum(down, axis=axis, keepdims=True)
    return up, down


def list_blocks(mine, pairs, info):
    late = 2 * (SEQ - 1 - mine) + 1
    odd = lax.rem(mine, 2)
    for slot in range(SLOTS):
        info[slot] = 0
    info[0] = 2 * mine
    info[2] = late
    late_first = 4 + 2 * (mine // 2)

    def scan(row, counts):
        early_count, late_count = counts
        query = pairs[2 * row]
        key = pairs[2 * row + 1]
        earlier = query != key
        is_early = (query == 2 * mine) & earlier
        is_late = (query == late) & earlier

        @pl.when(is_early | is_late)
        def _():
            early_slot = jnp.where(early_count < odd, 1, 4 + early_count - odd)
            late_slot = jnp.where(late_count < 1 - odd, 3, late_first + late_count - (1 - odd))
            info[jnp.minimum(jnp.where(is_early, early_slot, late_slot), SLOTS - 1)] = key

        return (
            early_count + jnp.where(is_early, 1, 0),
            late_count + jnp.where(is_late, 1, 0),
        )

    lax.fori_loop(0, pairs.shape[0] // 2, scan, (jnp.int32(0), jnp.int32(0)))
    info[32] = jnp.where(odd == 1, 2 * BLK, -2 * BLK)
    info[33] = jnp.where(odd == 1, -2 * BLK, 2 * BLK)
    info[34] = 2 + mine // 2
    info[35] = odd


def features(q, q_map_t, q_t, mapped_t, mapped, soft_t):
    for head in range(HEADS):
        lanes = pl.ds(head * BLK, BLK)
        rows_t = q[head].T
        q_t[:, lanes] = rows_t
        up, down = halves(dot(q_map_t[head], rows_t), 0)
        soft = jnp.concatenate([up, down], axis=0)
        soft_t[:, lanes] = soft
        rounded = soft.astype(BF16)
        mapped_t[:, lanes] = rounded
        mapped[lanes, :] = rounded.T


def list_kernel(place, pairs, info):
    list_blocks(place[0], pairs, info)


def main_kernel(
    info, same, other, k_map, early, late, q_map_t,
    near_out, far_out,
    q_t, mapped_t, mapped, soft_t, kv, v_t, k_t, soft_k, mk, mk_t,
    t_acc, s_acc, m_acc, l_acc, n_acc, gn, gnorm, gqf, gk_acc, flat, loss_acc,
    s_buf, x_raw, p_buf, x_buf, kf_buf, mk_next, v_next, shift_buf,
):
    parity = info[35]
    switch = info[34]

    def fetch(slot):
        block = info[slot]
        chip = block // 4
        rows = pl.ds(pl.multiple_of(lax.rem(block, 2) * BLK, BLK), BLK)
        near = lax.rem(block // 2, 2) == parity
        kv[slot] = jnp.where(near, same[chip, rows], other[chip, rows])

    def key_rows(step):
        return jnp.concatenate([kv[2 * step, :, :HD], kv[2 * step + 1, :, :HD]], axis=0)

    def value_rows(step):
        return jnp.concatenate([kv[2 * step, :, HD:], kv[2 * step + 1, :, HD:]], axis=0)

    def prepare(step):
        keys = key_rows(step)
        up, down = halves(dot(keys, k_map[...]), 1)
        soft_k[step, :, :HD] = up
        soft_k[step, :, HD:] = down
        up = up.astype(BF16)
        down = down.astype(BF16)
        mk_next[:, :HD] = up
        mk_next[:, HD:] = down
        mk_t[step, :HD] = up.T
        mk_t[step, HD:] = down.T
        v_next[...] = value_rows(step).T
        k_t[step] = keys.T

    def advance():
        mk[...] = mk_next[...]
        v_t[...] = v_next[...]

    def allowed_of(side):
        key_minus_query = lax.broadcasted_iota(jnp.int32, (BLK, BLK), 0) - (
            lax.broadcasted_iota(jnp.int32, (BLK, BLK), 1)
        )
        tall = jnp.concatenate(
            [key_minus_query <= 0, key_minus_query <= info[32 + side]], axis=0
        )
        return jnp.concatenate([tall, tall], axis=1)

    shrink = LOG2E / math.sqrt(HD)
    wide = 2 * BLK
    chunks = HEADS // 2

    tile = 64

    def over_sublanes(x, fold):
        return fold(x.reshape(x.shape[0] // 8, 8, x.shape[1]), axis=0)

    def forward(step, side, first, later):
        allowed = allowed_of(side) if first else None
        keys = key_rows(step)
        for c in range(chunks):
            lanes = pl.ds(c * wide, wide)
            s_buf[:, lanes] = dot(keys, q_t[side, :, lanes])
        for c in range(chunks):
            lanes = pl.ds(c * wide, wide)
            x_raw[:, lanes] = dot(mk[...], mapped_t[side, :, lanes])
        prepare(later)

        def masked(part, row, other):
            return jnp.where(allowed[row : row + tile], part, other) if first else part

        for c in range(chunks):
            lanes = pl.ds(c * wide, wide)
            best = jnp.full((8, wide), FLOOR, F32)
            for row in range(0, 2 * BLK, tile):
                part = masked(s_buf[pl.ds(row, tile), lanes], row, FLOOR)
                best = jnp.maximum(best, over_sublanes(part, jnp.max))
            new = jnp.max(best, axis=0, keepdims=True)
            if first:
                m_acc[side, c] = new
            else:
                old = m_acc[side, c]
                new = jnp.maximum(old, new)
                m_acc[side, c] = new
                shift = jnp.exp2((old - new) * shrink)
                shift_buf[c] = shift
            total = jnp.zeros((8, wide), F32)
            for row in range(0, 2 * BLK, tile):
                part = masked(s_buf[pl.ds(row, tile), lanes], row, FLOOR)
                weights = jnp.exp2((part - new) * shrink)
                total = total + over_sublanes(weights, jnp.sum)
                p_buf[pl.ds(row, tile), lanes] = weights.astype(BF16)
            l_acc[side, c] = total if first else l_acc[side, c] * shift + total
        for c in range(chunks):
            lanes = pl.ds(c * wide, wide)
            total = jnp.zeros((8, wide), F32)
            for row in range(0, 2 * BLK, tile):
                part = masked(x_raw[pl.ds(row, tile), lanes], row, 0.0)
                total = total + over_sublanes(part, jnp.sum)
                x_buf[pl.ds(row, tile), lanes] = part.astype(BF16)
            n_acc[side, c] = total if first else n_acc[side, c] + total
        for c in range(chunks):
            lanes = pl.ds(c * wide, wide)
            product = dot(v_t[...], x_buf[:, lanes])
            s_acc[side, c] = product if first else s_acc[side, c] + product
        for c in range(chunks):
            lanes = pl.ds(c * wide, wide)
            product = dot(v_t[...], p_buf[:, lanes])
            t_acc[side, c] = product if first else t_acc[side, c] * shift_buf[c] + product
        advance()

    def side_of(step):
        return jnp.where(step >= switch, 1, 0)

    for slot in range(SLOTS):
        fetch(slot)
    prepare(0)
    advance()
    for side, rows in enumerate((early, late)):
        features(rows, q_map_t, q_t.at[side], mapped_t.at[side], mapped.at[side], soft_t.at[side])
    forward(0, 0, True, 1)
    forward(1, 1, True, 2)

    def forward_turn(step, carry):
        forward(step, side_of(step), False, jnp.minimum(step + 1, STEPS - 1))
        return carry

    lax.fori_loop(2, STEPS, forward_turn, 0, unroll=UNROLL)

    def settle(side, loss):
        for c in range(chunks):
            norm = 1.0 / jnp.sum(n_acc[side, c], axis=0, keepdims=True)
            student = s_acc[side, c] * norm
            mass = 1.0 / jnp.sum(l_acc[side, c], axis=0, keepdims=True)
            mismatch = student - t_acc[side, c] * mass
            upstream = 2.0 * mismatch
            gn[side, c] = (upstream * norm).astype(BF16)
            gnorm[side, c] = -jnp.sum(upstream * student, axis=0, keepdims=True) * norm
            loss = loss + jnp.sum(mismatch * mismatch, axis=0, keepdims=True)
        return loss

    loss = lax.fori_loop(0, 2, settle, jnp.zeros((1, wide), F32))
    loss_acc[...] = jnp.broadcast_to(loss[:, :BLK] + loss[:, BLK:], loss_acc.shape)

    def key_back(step):
        grad_kf = kf_buf[...]
        soft = soft_k[step]
        lead, trail = soft[:, :HD], soft[:, HD:]
        g_lead, g_trail = grad_kf[:, :HD], grad_kf[:, HD:]
        back = lead * (g_lead - jnp.sum(lead * g_lead, axis=1, keepdims=True)) - trail * (
            g_trail - jnp.sum(trail * g_trail, axis=1, keepdims=True)
        )
        high, low = split_bf16(back)
        return dot(k_t[step], high) + dot(k_t[step], low)

    def backward(step, side, first):
        allowed = allowed_of(side) if first else None
        values = value_rows(step)
        for c in range(chunks):
            lanes = pl.ds(c * wide, wide)
            s_buf[:, lanes] = dot(values, gn[side, c])
        for c in range(chunks):
            lanes = pl.ds(c * wide, wide)
            for row in range(0, 2 * BLK, tile):
                part = s_buf[pl.ds(row, tile), lanes] + gnorm[side, c]
                if first:
                    part = jnp.where(allowed[row : row + tile], part, 0.0)
                p_buf[pl.ds(row, tile), lanes] = part.astype(BF16)
        for c in range(chunks):
            lanes = pl.ds(c * wide, wide)
            product = dot(mk_t[step], p_buf[:, lanes])
            gqf[side, c] = product if first else gqf[side, c] + product
        kf_buf[...] = dot(p_buf[...], mapped[side])

    backward(0, 0, True)
    gk_acc[...] = key_back(0)
    backward(1, 1, True)

    def backward_turn(step, carry):
        gk_acc[...] = gk_acc[...] + key_back(step - 1)
        backward(step, side_of(step), False)
        return carry

    lax.fori_loop(2, STEPS, backward_turn, 0, unroll=UNROLL)
    flat[pl.ds(HEADS * HD, HD)] = gk_acc[...] + key_back(STEPS - 1)

    for head in range(HEADS):
        total = jnp.zeros((HD, HD), F32)
        lanes = pl.ds(head * BLK, BLK)
        column = (head % 2) * BLK
        for side in range(2):
            lead, trail = soft_t[side, :HD, lanes], soft_t[side, HD:, lanes]
            g_lead = gqf[side, head // 2, :HD, pl.ds(column, BLK)]
            g_trail = gqf[side, head // 2, HD:, pl.ds(column, BLK)]
            back = lead * (g_lead - jnp.sum(lead * g_lead, axis=0, keepdims=True)) - trail * (
                g_trail - jnp.sum(trail * g_trail, axis=0, keepdims=True)
            )
            high, low = split_bf16(back)
            rows_t = q_t[side, :, lanes]
            total = total + dot_nt(rows_t, high) + dot_nt(rows_t, low)
        flat[pl.ds(head * HD, HD)] = total
    loss_row = loss_acc[:1]
    high, low = split_bf16(loss_row)
    rest = jnp.zeros((6, BLK), F32)
    near_tail = jnp.concatenate([loss_row, jnp.zeros((1, BLK), F32), rest], axis=0)
    far_tail = jnp.concatenate([high, low, rest.astype(BF16)], axis=0)
    for chip in range(CHIPS):
        near_row = pl.multiple_of((parity * CHIPS + chip) * ROWS, 8)
        far_row = pl.multiple_of(((1 - parity) * CHIPS + chip) * ROWS, 8)
        near_out[chip, pl.ds(0, ROWS)] = flat[pl.ds(near_row, ROWS)]
        near_out[chip, pl.ds(ROWS, PAYLOAD - ROWS)] = near_tail
        far_out[chip, pl.ds(0, ROWS)] = flat[pl.ds(far_row, ROWS)].astype(BF16)
        far_out[chip, pl.ds(ROWS, PAYLOAD - ROWS)] = far_tail


def fold_kernel(pieces, chunk, stats):
    total = jnp.sum(pieces[...].astype(F32), axis=0)
    grads = total[:ROWS]
    chunk[...] = grads.astype(BF16)
    squares = jnp.sum(grads * grads, axis=0, keepdims=True)
    loss = total[ROWS : ROWS + 1] + total[ROWS + 1 : ROWS + 2]
    rows = jnp.concatenate([squares, loss, jnp.zeros((6, BLK), F32)], axis=0)
    for peer in range(KV):
        stats[peer] = rows


def share_kernel(chunk, stats, payload, loss):
    total = jnp.sum(stats[...], axis=0)
    high, low = split_bf16(total)
    tail = jnp.concatenate([high[:1], low[:1], jnp.zeros((6, BLK), BF16)], axis=0)
    for peer in range(CHIPS):
        payload[peer, pl.ds(0, ROWS)] = chunk[...]
        payload[peer, pl.ds(ROWS, PAYLOAD - ROWS)] = tail
    loss[...] = jnp.broadcast_to(
        jnp.sum(total[1:2], axis=1, keepdims=True) / (SEQ * 2 * BLK * KV * HEADS * HD), loss.shape
    )


def scale_kernel(place, own, sibling, q_out, k_out):
    south = lax.rem(place[0], 2) == 0
    heads = HEADS * HD
    sides = (
        jnp.where(south, own[...], sibling[...]),
        jnp.where(south, sibling[...], own[...]),
    )
    squared = jnp.zeros((1, BLK), F32)
    for side in sides:
        tail = side[:, ROWS:, :].astype(F32)
        squared = squared + jnp.sum(tail[:, 0, :] + tail[:, 1, :], axis=0, keepdims=True)
    squared = jnp.sum(squared, axis=1, keepdims=True)
    inverse = 1.0 / jnp.sqrt(squared / ((HEADS + 1) * KV * HD * HD) + 1e-06)
    for piece in range(SEQ):
        rows = sides[piece // CHIPS][piece % CHIPS, :ROWS].astype(F32) * inverse
        first = piece * ROWS
        keep = min(max(heads - first, 0), ROWS)
        if keep:
            q_out[pl.ds(first, keep)] = rows[:keep]
        if keep < ROWS:
            k_out[pl.ds(first + keep - heads, ROWS - keep)] = rows[keep:]


def pack_kernel(keys, values, out, both, sems):
    takes = [
        pltpu.make_async_copy(keys, both.at[:, pl.ds(0, HD)], sems.at[0]),
        pltpu.make_async_copy(values, both.at[:, pl.ds(HD, HD)], sems.at[1]),
    ]
    for take in takes:
        take.start()
    for take in takes:
        take.wait()
    gives = [
        pltpu.make_async_copy(both, out.at[peer], sems.at[2 + peer]) for peer in range(CHIPS)
    ]
    for give in gives:
        give.start()
    for give in gives:
        give.wait()


def vmem():
    return pl.BlockSpec(memory_space=pltpu.VMEM)


def smem():
    return pl.BlockSpec(memory_space=pltpu.SMEM)


def shape(dims, kind):
    return jax.ShapeDtypeStruct(dims, kind)


def attend(info, same, other, k_map, early, late, q_map_t):
    wide = HEADS * BLK
    pair = 2 * BLK
    chunks = HEADS // 2
    return pl.pallas_call(
        main_kernel,
        out_shape=(shape((CHIPS, PAYLOAD, BLK), F32), shape((CHIPS, PAYLOAD, BLK), BF16)),
        in_specs=[smem()] + [vmem()] * 6,
        out_specs=(vmem(), vmem()),
        scratch_shapes=[
            pltpu.VMEM((2, HD, wide), BF16),
            pltpu.VMEM((2, 2 * HD, wide), BF16),
            pltpu.VMEM((2, wide, 2 * HD), BF16),
            pltpu.VMEM((2, 2 * HD, wide), F32),
            pltpu.VMEM((SLOTS, BLK, 2 * HD), BF16),
            pltpu.VMEM((HD, pair), BF16),
            pltpu.VMEM((STEPS, HD, pair), BF16),
            pltpu.VMEM((STEPS, pair, 2 * HD), F32),
            pltpu.VMEM((pair, 2 * HD), BF16),
            pltpu.VMEM((STEPS, 2 * HD, pair), BF16),
            pltpu.VMEM((2, chunks, HD, pair), F32),
            pltpu.VMEM((2, chunks, HD, pair), F32),
            pltpu.VMEM((2, chunks, 1, pair), F32),
            pltpu.VMEM((2, chunks, 8, pair), F32),
            pltpu.VMEM((2, chunks, 8, pair), F32),
            pltpu.VMEM((2, chunks, HD, pair), BF16),
            pltpu.VMEM((2, chunks, 1, pair), F32),
            pltpu.VMEM((2, chunks, 2 * HD, pair), F32),
            pltpu.VMEM((HD, HD), F32),
            pltpu.VMEM(((HEADS + 1) * HD, HD), F32),
            pltpu.VMEM((8, BLK), F32),
            pltpu.VMEM((pair, wide), F32),
            pltpu.VMEM((pair, wide), F32),
            pltpu.VMEM((pair, wide), BF16),
            pltpu.VMEM((pair, wide), BF16),
            pltpu.VMEM((pair, 2 * HD), F32),
            pltpu.VMEM((pair, 2 * HD), BF16),
            pltpu.VMEM((HD, pair), BF16),
            pltpu.VMEM((chunks, 1, pair), F32),
        ],
        compiler_params=pltpu.CompilerParams(vmem_limit_bytes=ATTEND_VMEM),
        name="attend",
    )(info, same, other, k_map, early, late, q_map_t)


def layer(queries, keys, values, q_map, k_map, block_pairs):
    place = lax.axis_index("seq").astype(jnp.int32).reshape(1)
    sent = pl.pallas_call(
        pack_kernel,
        out_shape=shape((CHIPS, 2 * BLK, 2 * HD), BF16),
        in_specs=[pl.BlockSpec(memory_space=pl.ANY)] * 2,
        out_specs=pl.BlockSpec(memory_space=pl.ANY),
        scratch_shapes=[
            pltpu.VMEM((2 * BLK, 2 * HD), BF16),
            pltpu.SemaphoreType.DMA((2 + CHIPS,)),
        ],
        compiler_params=pltpu.CompilerParams(vmem_limit_bytes=56 * 1024 * 1024),
        name="pack",
    )(keys[:, 0, :], values[:, 0, :])
    same = lax.all_to_all(sent, "seq", 0, 0, axis_index_groups=SAME_CORE, tiled=True)
    other = lax.ppermute(same, "seq", OTHER_CORE)

    early = jnp.transpose(queries[:BLK], (1, 0, 2))
    late = jnp.transpose(queries[BLK:], (1, 0, 2))
    late = lax.ppermute(late, "seq", MIRROR)
    q_map_t = jnp.transpose(q_map, (0, 2, 1))
    info = pl.pallas_call(
        list_kernel,
        out_shape=shape((128,), jnp.int32),
        in_specs=[smem(), smem()],
        out_specs=smem(),
        cost_estimate=pl.CostEstimate(flops=5 * 10**9, bytes_accessed=10**5, transcendentals=0),
        compiler_params=pltpu.CompilerParams(vmem_limit_bytes=SMALL_VMEM),
        name="list",
    )(place, block_pairs.reshape(-1))

    small = pltpu.CompilerParams(vmem_limit_bytes=SMALL_VMEM)
    near, far = attend(info, same, other, k_map[0], early, late, q_map_t)
    met = (near + lax.ppermute(far, "seq", OTHER_CORE).astype(F32)).astype(BF16)
    pieces = lax.all_to_all(met, "seq", 0, 0, axis_index_groups=SAME_CORE, tiled=True)
    chunk, stats = pl.pallas_call(
        fold_kernel,
        out_shape=(shape((ROWS, BLK), BF16), shape((KV, 8, BLK), F32)),
        in_specs=[vmem()],
        out_specs=(vmem(), vmem()),
        compiler_params=small,
        name="fold",
    )(pieces)
    stats = lax.all_to_all(stats, "kv", 0, 0, tiled=True)
    payload, loss = pl.pallas_call(
        share_kernel,
        out_shape=(shape((CHIPS, PAYLOAD, BLK), BF16), shape((8, BLK), F32)),
        in_specs=[vmem(), vmem()],
        out_specs=(vmem(), vmem()),
        compiler_params=small,
        name="share",
    )(chunk, stats)
    own = lax.all_to_all(payload, "seq", 0, 0, axis_index_groups=SAME_CORE, tiled=True)
    sibling = lax.ppermute(own, "seq", OTHER_CORE)
    grad_q, grad_k = pl.pallas_call(
        scale_kernel,
        out_shape=(shape((HEADS * HD, HD), F32), shape((HD, HD), F32)),
        in_specs=[smem(), vmem(), vmem()],
        out_specs=(vmem(), vmem()),
        compiler_params=small,
        name="scale",
    )(place, own, sibling)
    return grad_q.reshape(HEADS, HD, HD), grad_k.reshape(1, HD, HD), loss[0, 0]


def solution(mesh):
    placed = (
        P("seq", "kv", None),
        P("seq", "kv", None),
        P("seq", "kv", None),
        P("kv", None, None),
        P("kv", None, None),
        P(),
    )
    return jax.shard_map(
        layer,
        mesh=mesh,
        in_specs=placed,
        out_specs=(P("kv", None, None), P("kv", None, None), P()),
        check_vma=False,
    )
```

time: 111 us -> 91.3 us (0.82)
  Pallas kernels: 38.4 us -> 25.1 us
  local copies, waits for them, and re-layouts: 8.04 us -> 1.1 us
  blocking collectives: 49.7 us -> 55.3 us
  starting transfers between devices: 5.21 us -> 2.27 us
  waiting for transfers between devices: 7.49 us -> 5.31 us
    pallas_call x4, Pallas kernels: 34.8 us -> 24.1 us  [the longest x1 17.6 us: attend(): pl.pallas_call(main_kernel, out_shape=(shape((CHIPS, PAYLOAD, BLK), F32),...]
    all_to_all x1 -> x0, waiting for transfers between devices: 7.49 us -> none  [layer(): shared = lax.all_to_all(payload, 'seq', 0, 0, tiled=True)]
    all_to_all x1 -> x2, blocking collectives: 12.9 us -> 18.7 us  [the longest x1 9.5 us: layer(): lax.all_to_all(met, 'seq', 0, 0, axis_index_groups=SAME_CORE, tiled=True)]
    ppermute x1 -> x3, waiting for transfers between devices: 0.01 us -> 5.31 us  [the longest x1 3.4 us: layer(): late = lax.ppermute(late, 'seq', MIRROR)]
    unnamed x18 -> x12, local copies, waits for them, and re-layouts: 4.25 us -> 0.41 us
    all_to_all x1 -> x0, starting transfers between devices: 3.54 us -> none  [layer(): shared = lax.all_to_all(payload, 'seq', 0, 0, tiled=True)]
    broadcast_in_dim x2 -> x0, local copies, waits for them, and re-layouts: 1.82 us -> none  [the longest x1 0.91 us: layer(): jnp.broadcast_to(values[:, 0, :], many)]
    pallas_call x1, Pallas kernels: 1.65 us -> 0.04 us  [layer(): pl.pallas_call(fold_kernel, out_shape=(shape((ROWS, BLK), BF16), shape((K...]
  transfers between devices with their start and end apart: 3 -> 4, of which waited for: 1 -> 3; matrix products, arithmetic and copies ran while one was open for 3% -> 1% of each run, Pallas kernels for 8% -> 5%
where the time goes in v2:
time: 91.3 us; the launch traced here: 89.9 us
  blocking collectives  55.3 us (61%)
  Pallas kernels  25.1 us (27%)
  waiting for transfers between devices  5.31 us (6%)
  starting transfers between devices  2.27 us (2%)
  local copies, waits for them, and re-layouts  1.1 us (1%)
    all_to_all x1, blocking collectives, layer(): lax.all_to_all(sent, 'seq', 0, 0, axis_index_groups=SAME_CORE, tiled=True)  22.4 us
    pallas_call x1, Pallas kernels, attend(): pl.pallas_call(main_kernel, out_shape=(shape((CHIPS, PAYLOAD, BLK), F32),...  17.6 us
    all_to_all x1, blocking collectives, layer(): stats = lax.all_to_all(stats, 'kv', 0, 0, tiled=True)  14.2 us
    all_to_all x1, blocking collectives, layer(): lax.all_to_all(met, 'seq', 0, 0, axis_index_groups=SAME_CORE, tiled=True)  9.5 us
    all_to_all x1, blocking collectives, layer(): lax.all_to_all(payload, 'seq', 0, 0, axis_index_groups=SAME_CORE, tiled=T...  9.21 us
    pallas_call x1, Pallas kernels, layer(): pl.pallas_call(list_kernel, out_shape=shape((128,), jnp.int32), in_specs=...  4.48 us
    ppermute x1, waiting for transfers between devices, layer(): late = lax.ppermute(late, 'seq', MIRROR)  3.4 us
    pallas_call x1, Pallas kernels, layer(): pl.pallas_call(pack_kernel, out_shape=shape((CHIPS, 2 * BLK, 2 * HD), BF1...  1.93 us
  transfers between devices with their start and end apart: 4, of which 3 were waited for; matrix products, arithmetic and copies ran while one was open for 1% of the time, Pallas kernels for 5%

profile of v2, /device:TPU:0, one launch (start us, length us, event | category | flops | bytes accessed | tf_op | source)
XLA Modules:
  0.0 89.9 jit_solution(8899004195166827213)
XLA Ops:
  0.6 1.9 %pack.1 = bf16[8,256,256]{2,1,0:T(8,128)(2,1)} custom-call(bf16[256,128]{1,0:T(8,128)(2,1)} %bitcast.18, bf16[256,128]{1,0:T(8,128)(2,1)} %bitcast.19), custom_call_target="tpu_custom_call" | custom-call | tf_op jit(solution)/shard_map/pack/pallas_call | solution.py:449
  2.6 0.0 copy-start.1
  2.6 22.4 %all_to_all.20.same = bf16[8,256,256]{2,1,0:T(8,128)(2,1)S(1)} all-to-all(bf16[8,256,256]{2,1,0:T(8,128)(2,1)} %pack.1), channel_id=1, replica_groups={{0,16,32,48,64,80,96,112},{8,24,40,56,72,88,104,120},{1,17,33,49,65,81,..., dimensions={0} | all-to-all | bytes 2097152 | tf_op jit(solution)/shard_map/all_to_all | solution.py:461
  25.0 0.0 collective-permute-start
  25.0 0.0 copy-done.1
  25.0 0.0 copy-start.3
  25.1 0.0 copy-start.2
  25.1 1.7 %collective-permute-start.1 = (bf16[8,128,128]{2,1,0:T(8,128)(2,1)S(1)}, bf16[8,128,128]{2,1,0:T(8,128)(2,1)S(1)}, u32[]{:S(2)}, u32[]{:S(2)}) collective-permute-start(bf16[8,128,128]{2,1,0:T(8,128)(2,1)S(1)} %bitcast.17), channel_id=1, source_target_pairs={{0,120},{8,112},{16,104},{24,96},{32,88},{40,80},{48,72},{56,64},{... | collective-permute-start | bytes 786440 | tf_op jit(solution)/shard_map/ppermute | solution.py:466
  26.8 0.0 copy-done.3
  26.8 0.1 copy.12
  26.9 0.1 reshape.19.pairs
  27.1 0.0 copy-done.2
  27.1 0.2 copy.15
  27.3 0.0 copy-start
  27.3 4.5 %list.1.info = s32[128]{0:T(128)S(1)} custom-call(s32[1]{0:T(128)} %bitcast.place, s32[544]{0:T(1024)S(1)} %reshape.19.pairs), custom_call_target="tpu_custom_call" | custom-call | flops 5000000000 | bytes 100000 | tf_op jit(solution)/shard_map/list/pallas_call | solution.py:468
  31.8 3.4 %collective-permute-done.1.late = bf16[8,128,128]{2,1,0:T(8,128)(2,1)S(1)} collective-permute-done((bf16[8,128,128]{2,1,0:T(8,128)(2,1)S(1)}, bf16[8,128,128]{2,1,0:T(8,128)(2,1)S(1)}, u32[]{:S(2)}, u32[]{:S(2)}) %collective-permute-start.1) | collective-permute-done | bytes 262176 | tf_op jit(solution)/shard_map/ppermute | solution.py:466
  35.2 0.0 collective-permute-done.other
  35.2 0.0 copy-done
  35.2 17.6 %attend.1 = (f32[8,80,128]{2,1,0:T(8,128)S(1)}, bf16[8,80,128]{2,1,0:T(8,128)(2,1)S(1)}) custom-call(s32[128]{0:T(128)S(1)} %list.1.info, bf16[8,256,256]{2,1,0:T(8,128)(2,1)S(1)} %all_to_all.20.same, bf16[8,256,256]{2,1,0:T(8,128)(2,1)S(1)} %collective-permute-done.other, bf16[128,128]{1,0:T(8,128)(2,1)S(1)} %bitcast.16, bf16[8,128,128]{2,1,0:T(8,128)(2,1)S(1)} %bitcast.15, ...), custom_call_target="tpu_custom_call" | custom-call | tf_op jit(solution)/shard_map/attend/pallas_call | solution.py:406
  52.9 0.6 collective-permute-start.2
  53.5 1.0 %collective-permute-done.2 = bf16[8,80,128]{2,1,0:T(8,128)(2,1)S(1)} collective-permute-done((bf16[8,80,128]{2,1,0:T(8,128)(2,1)S(1)}, bf16[8,80,128]{2,1,0:T(8,128)(2,1)S(1)}, u32[]{:S(2)}, u32[]{:S(2)}) %collective-permute-start.2) | collective-permute-done | bytes 163872 | tf_op jit(solution)/shard_map/ppermute | solution.py:480
  54.5 9.5 %all_to_all.21.pieces = bf16[8,80,128]{2,1,0:T(8,128)(2,1)S(1)} all-to-all(bf16[8,80,128]{2,1,0:T(8,128)(2,1)S(1)} %add_convert_fusion), channel_id=1, replica_groups={{0,16,32,48,64,80,96,112},{8,24,40,56,72,88,104,120},{1,17,33,49,65,81,..., dimensions={0} | all-to-all | bytes 327680 | tf_op jit(solution)/shard_map/all_to_all | solution.py:481
  64.1 14.2 %all_to_all.22.stats = f32[8,8,128]{2,1,0:T(8,128)S(1)} all-to-all(f32[8,8,128]{2,1,0:T(8,128)S(1)} %get-tuple-element.14), channel_id=1, replica_groups=mesh['seq'=16,'kv'=8] {'kv'}, dimensions={0} | all-to-all | bytes 65536 | tf_op jit(solution)/shard_map/all_to_all | solution.py:490
  78.3 0.1 share.1
  78.3 9.2 %all_to_all.23.own = bf16[8,80,128]{2,1,0:T(8,128)(2,1)S(1)} all-to-all(bf16[8,80,128]{2,1,0:T(8,128)(2,1)S(1)} %get-tuple-element.15), channel_id=1, replica_groups={{0,16,32,48,64,80,96,112},{8,24,40,56,72,88,104,120},{1,17,33,49,65,81,..., dimensions={0} | all-to-all | bytes 327680 | tf_op jit(solution)/shard_map/all_to_all | solution.py:499
  87.6 0.0 collective-permute-start.3
  87.6 0.5 slice.11
  88.1 0.9 collective-permute-done.3.sibling
  89.0 1.0 %scale.1 = (f32[1024,128]{1,0:T(8,128)}, f32[128,128]{1,0:T(8,128)}) custom-call(s32[1]{0:T(128)} %bitcast.place, bf16[8,80,128]{2,1,0:T(8,128)(2,1)S(1)} %all_to_all.23.own, bf16[8,80,128]{2,1,0:T(8,128)(2,1)S(1)} %collective-permute-done.3.sibling), custom_call_target="tpu_custom_call" | custom-call | tf_op jit(solution)/shard_map/scale/pallas_call | solution.py:501
  (5 shorter events, 0.2 us)
Async XLA Ops:
  2.6 22.4 %copy-start.1 = (bf16[256,8,128]{2,1,0:T(8,128)(2,1)S(1)}, bf16[256,8,128]{2,1,0:T(8,128)(2,1)}, u32[]{:S(2)}) copy-start(bf16[256,8,128]{2,1,0:T(8,128)(2,1)} %param.6) | copy-start | bytes 1572868
  25.0 10.2 %collective-permute-start = (bf16[8,256,256]{2,1,0:T(8,128)(2,1)S(1)}, bf16[8,256,256]{2,1,0:T(8,128)(2,1)S(1)}, u32[]{:S(2)}, u32[]{:S(2)}) collective-permute-start(bf16[8,256,256]{2,1,0:T(8,128)(2,1)S(1)} %all_to_all.20.same), channel_id=1, source_target_pairs={{0,8},{8,0},{16,24},{24,16},{32,40},{40,32},{48,56},{56,48},{64,72... | collective-permute-start | bytes 3145736 | tf_op jit(solution)/shard_map/ppermute | solution.py:462
  25.0 1.7 %copy-start.3 = (s32[272,2]{0,1:T(2,128)S(1)}, s32[272,2]{0,1:T(2,128)}, u32[]{:S(2)}) copy-start(s32[272,2]{0,1:T(2,128)} %param.11) | copy-start | bytes 6532
  25.1 2.0 %copy-start.2 = (bf16[8,128,128]{2,1,0:T(8,128)(2,1)S(1)}, bf16[8,128,128]{2,1,0:T(8,128)(2,1)}, u32[]{:S(2)}) copy-start(bf16[8,128,128]{2,1,0:T(8,128)(2,1)} %param.9) | copy-start | bytes 786436
  25.1 10.1 %collective-permute-start.1 = (bf16[8,128,128]{2,1,0:T(8,128)(2,1)S(1)}, bf16[8,128,128]{2,1,0:T(8,128)(2,1)S(1)}, u32[]{:S(2)}, u32[]{:S(2)}) collective-permute-start(bf16[8,128,128]{2,1,0:T(8,128)(2,1)S(1)} %bitcast.17), channel_id=1, source_target_pairs={{0,120},{8,112},{16,104},{24,96},{32,88},{40,80},{48,72},{56,64},{... | collective-permute-start | bytes 786440 | tf_op jit(solution)/shard_map/ppermute | solution.py:466
  27.3 7.9 %copy-start = (bf16[1,128,128]{2,1,0:T(8,128)(2,1)S(1)}, bf16[1,128,128]{2,1,0:T(8,128)(2,1)}, u32[]{:S(2)}) copy-start(bf16[1,128,128]{2,1,0:T(8,128)(2,1)} %param.10) | copy-start | bytes 98308
  52.9 1.6 %collective-permute-start.2 = (bf16[8,80,128]{2,1,0:T(8,128)(2,1)S(1)}, bf16[8,80,128]{2,1,0:T(8,128)(2,1)S(1)}, u32[]{:S(2)}, u32[]{:S(2)}) collective-permute-start(bf16[8,80,128]{2,1,0:T(8,128)(2,1)S(1)} %get-tuple-element.12), channel_id=1, source_target_pairs={{0,8},{8,0},{16,24},{24,16},{32,40},{40,32},{48,56},{56,48},{64,72... | collective-permute-start | bytes 491528 | tf_op jit(solution)/shard_map/ppermute | solution.py:480
  87.6 1.4 %collective-permute-start.3 = (bf16[8,80,128]{2,1,0:T(8,128)(2,1)S(1)}, bf16[8,80,128]{2,1,0:T(8,128)(2,1)S(1)}, u32[]{:S(2)}, u32[]{:S(2)}) collective-permute-start(bf16[8,80,128]{2,1,0:T(8,128)(2,1)S(1)} %all_to_all.23.own), channel_id=1, source_target_pairs={{0,8},{8,0},{16,24},{24,16},{32,40},{40,32},{48,56},{56,48},{64,72... | collective-permute-start | bytes 491528 | tf_op jit(solution)/shard_map/ppermute | solution.py:500

commit v3 on v2

--- a/solution.py
+++ b/solution.py
@@ -16,8 +16,7 @@
 CHIPS = SEQ // 2
 SLOTS = 18
 STEPS = SLOTS // 2
-UNROLL = 7
-ATTEND_VMEM = 26 * 1024 * 1024
+ATTEND_VMEM = 34 * 1024 * 1024
 SMALL_VMEM = 4 * 1024 * 1024
 FLOOR = -1e30
 LOG2E = 1.4426950408889634
@@ -28,6 +27,8 @@
 
 SAME_CORE = [[core + 2 * chip for chip in range(SEQ // 2)] for core in range(2)]
 OTHER_CORE = [(i, i ^ 1) for i in range(SEQ)]
+OTHER_ROW = [(i, i ^ 2) for i in range(SEQ)]
+LAYER_SHIFTS = [[(i, (i + 4 * back) % SEQ) for i in range(SEQ)] for back in (1, 2, 3)]
 MIRROR = [(i, SEQ - 1 - i) for i in range(SEQ)]
 
 
@@ -111,7 +112,7 @@
     near_out, far_out,
     q_t, mapped_t, mapped, soft_t, kv, v_t, k_t, soft_k, mk, mk_t,
     t_acc, s_acc, m_acc, l_acc, n_acc, gn, gnorm, gqf, gk_acc, flat, loss_acc,
-    s_buf, x_raw, p_buf, x_buf, kf_buf, mk_next, v_next, shift_buf,
+    s_bufs, x_raws, p_bufs, x_bufs, kf_bufs, shift_bufs,
 ):
     parity = info[35]
     switch = info[34]
@@ -136,16 +137,12 @@
         soft_k[step, :, HD:] = down
         up = up.astype(BF16)
         down = down.astype(BF16)
-        mk_next[:, :HD] = up
-        mk_next[:, HD:] = down
+        mk[step, :, :HD] = up
+        mk[step, :, HD:] = down
         mk_t[step, :HD] = up.T
         mk_t[step, HD:] = down.T
-        v_next[...] = value_rows(step).T
+        v_t[step] = value_rows(step).T
         k_t[step] = keys.T
-
-    def advance():
-        mk[...] = mk_next[...]
-        v_t[...] = v_next[...]
 
     def allowed_of(side):
         key_minus_query = lax.broadcasted_iota(jnp.int32, (BLK, BLK), 0) - (
@@ -165,16 +162,28 @@
     def over_sublanes(x, fold):
         return fold(x.reshape(x.shape[0] // 8, 8, x.shape[1]), axis=0)
 
-    def forward(step, side, first, later):
+    def side_of(step):
+        if step < 2:
+            return step
+        return jnp.where(step >= switch, 1, 0)
+
+    def forward_dots(step):
+        side = side_of(step)
+        s_buf, x_raw = s_bufs.at[step % 2], x_raws.at[step % 2]
+        keys = key_rows(step)
+        for c in range(chunks):
+            lanes = pl.ds(c * wide, wide)
+            s_buf[:, lanes] = dot(keys, q_t[side, :, lanes])
+        for c in range(chunks):
+            lanes = pl.ds(c * wide, wide)
+            x_raw[:, lanes] = dot(mk[step], mapped_t[side, :, lanes])
+
+    def forward(step):
+        side, first = side_of(step), step < 2
         allowed = allowed_of(side) if first else None
-        keys = key_rows(step)
-        for c in range(chunks):
-            lanes = pl.ds(c * wide, wide)
-            s_buf[:, lanes] = dot(keys, q_t[side, :, lanes])
-        for c in range(chunks):
-            lanes = pl.ds(c * wide, wide)
-            x_raw[:, lanes] = dot(mk[...], mapped_t[side, :, lanes])
-        prepare(later)
+        s_buf, x_raw = s_bufs.at[step % 2], x_raws.at[step % 2]
+        p_buf, x_buf = p_bufs.at[step % 2], x_bufs.at[step % 2]
+        shift_buf = shift_bufs.at[step % 2]
 
         def masked(part, row, other):
             return jnp.where(allowed[row : row + tile], part, other) if first else part
@@ -211,31 +220,26 @@
             n_acc[side, c] = total if first else n_acc[side, c] + total
         for c in range(chunks):
             lanes = pl.ds(c * wide, wide)
-            product = dot(v_t[...], x_buf[:, lanes])
+            product = dot(v_t[step], x_buf[:, lanes])
             s_acc[side, c] = product if first else s_acc[side, c] + product
         for c in range(chunks):
             lanes = pl.ds(c * wide, wide)
-            product = dot(v_t[...], p_buf[:, lanes])
+            product = dot(v_t[step], p_buf[:, lanes])
             t_acc[side, c] = product if first else t_acc[side, c] * shift_buf[c] + product
-        advance()
-
-    def side_of(step):
-        return jnp.where(step >= switch, 1, 0)
 
     for slot in range(SLOTS):
         fetch(slot)
     prepare(0)
-    advance()
     for side, rows in enumerate((early, late)):
         features(rows, q_map_t, q_t.at[side], mapped_t.at[side], mapped.at[side], soft_t.at[side])
-    forward(0, 0, True, 1)
-    forward(1, 1, True, 2)
-
-    def forward_turn(step, carry):
-        forward(step, side_of(step), False, jnp.minimum(step + 1, STEPS - 1))
-        return carry
-
-    lax.fori_loop(2, STEPS, forward_turn, 0, unroll=UNROLL)
+    prepare(1)
+    forward_dots(0)
+    for step in range(STEPS):
+        if step + 2 < STEPS:
+            prepare(step + 2)
+        if step + 1 < STEPS:
+            forward_dots(step + 1)
+        forward(step)
 
     def settle(side, loss):
         for c in range(chunks):
@@ -253,7 +257,7 @@
     loss_acc[...] = jnp.broadcast_to(loss[:, :BLK] + loss[:, BLK:], loss_acc.shape)
 
     def key_back(step):
-        grad_kf = kf_buf[...]
+        grad_kf = kf_bufs[step % 2]
         soft = soft_k[step]
         lead, trail = soft[:, :HD], soft[:, HD:]
         g_lead, g_trail = grad_kf[:, :HD], grad_kf[:, HD:]
@@ -263,8 +267,10 @@
         high, low = split_bf16(back)
         return dot(k_t[step], high) + dot(k_t[step], low)
 
-    def backward(step, side, first):
+    def backward_dots(step):
+        side, first = side_of(step), step < 2
         allowed = allowed_of(side) if first else None
+        s_buf, p_buf = s_bufs.at[step % 2], p_bufs.at[step % 2]
         values = value_rows(step)
         for c in range(chunks):
             lanes = pl.ds(c * wide, wide)
@@ -276,22 +282,24 @@
                 if first:
                     part = jnp.where(allowed[row : row + tile], part, 0.0)
                 p_buf[pl.ds(row, tile), lanes] = part.astype(BF16)
+
+    def backward(step):
+        side, first = side_of(step), step < 2
+        p_buf = p_bufs.at[step % 2]
         for c in range(chunks):
             lanes = pl.ds(c * wide, wide)
             product = dot(mk_t[step], p_buf[:, lanes])
             gqf[side, c] = product if first else gqf[side, c] + product
-        kf_buf[...] = dot(p_buf[...], mapped[side])
-
-    backward(0, 0, True)
-    gk_acc[...] = key_back(0)
-    backward(1, 1, True)
-
-    def backward_turn(step, carry):
-        gk_acc[...] = gk_acc[...] + key_back(step - 1)
-        backward(step, side_of(step), False)
-        return carry
-
-    lax.fori_loop(2, STEPS, backward_turn, 0, unroll=UNROLL)
+        kf_bufs[step % 2] = dot(p_buf[...], mapped[side])
+
+    backward_dots(0)
+    gk_acc[...] = jnp.zeros((HD, HD), F32)
+    for step in range(STEPS):
+        if step + 1 < STEPS:
+            backward_dots(step + 1)
+        backward(step)
+        if step:
+            gk_acc[...] = gk_acc[...] + key_back(step - 1)
     flat[pl.ds(HEADS * HD, HD)] = gk_acc[...] + key_back(STEPS - 1)
 
     for head in range(HEADS):
@@ -328,45 +336,36 @@
     grads = total[:ROWS]
     chunk[...] = grads.astype(BF16)
     squares = jnp.sum(grads * grads, axis=0, keepdims=True)
-    loss = total[ROWS : ROWS + 1] + total[ROWS + 1 : ROWS + 2]
-    rows = jnp.concatenate([squares, loss, jnp.zeros((6, BLK), F32)], axis=0)
-    for peer in range(KV):
-        stats[peer] = rows
-
-
-def share_kernel(chunk, stats, payload, loss):
+    loss = (total[ROWS : ROWS + 1] + total[ROWS + 1 : ROWS + 2]) * (1.0 / SEQ)
+    half = BLK // 2
+    row = jnp.concatenate(
+        [squares[:, :half] + squares[:, half:], loss[:, :half] + loss[:, half:]], axis=1
+    )
+    stats[...] = jnp.broadcast_to(row[None], stats.shape)
+
+
+def scale_kernel(place, stats, near, across, far, far_across, q_out, k_out, loss, flat):
     total = jnp.sum(stats[...], axis=0)
-    high, low = split_bf16(total)
-    tail = jnp.concatenate([high[:1], low[:1], jnp.zeros((6, BLK), BF16)], axis=0)
-    for peer in range(CHIPS):
-        payload[peer, pl.ds(0, ROWS)] = chunk[...]
-        payload[peer, pl.ds(ROWS, PAYLOAD - ROWS)] = tail
-    loss[...] = jnp.broadcast_to(
-        jnp.sum(total[1:2], axis=1, keepdims=True) / (SEQ * 2 * BLK * KV * HEADS * HD), loss.shape
+    left = lax.broadcasted_iota(jnp.int32, (1, BLK), 1) < BLK // 2
+    squared = jnp.sum(jnp.where(left, total, 0.0), axis=1, keepdims=True)
+    loss[...] = jnp.sum(jnp.where(left, 0.0, total), axis=1, keepdims=True) / (
+        SEQ * 2 * BLK * KV * HEADS * HD
     )
-
-
-def scale_kernel(place, own, sibling, q_out, k_out):
-    south = lax.rem(place[0], 2) == 0
-    heads = HEADS * HD
-    sides = (
-        jnp.where(south, own[...], sibling[...]),
-        jnp.where(south, sibling[...], own[...]),
-    )
-    squared = jnp.zeros((1, BLK), F32)
-    for side in sides:
-        tail = side[:, ROWS:, :].astype(F32)
-        squared = squared + jnp.sum(tail[:, 0, :] + tail[:, 1, :], axis=0, keepdims=True)
-    squared = jnp.sum(squared, axis=1, keepdims=True)
     inverse = 1.0 / jnp.sqrt(squared / ((HEADS + 1) * KV * HD * HD) + 1e-06)
-    for piece in range(SEQ):
-        rows = sides[piece // CHIPS][piece % CHIPS, :ROWS].astype(F32) * inverse
-        first = piece * ROWS
-        keep = min(max(heads - first, 0), ROWS)
-        if keep:
-            q_out[pl.ds(first, keep)] = rows[:keep]
-        if keep < ROWS:
-            k_out[pl.ds(first + keep - heads, ROWS - keep)] = rows[keep:]
+    mine = place[0]
+    core = lax.rem(mine, 2)
+    row = lax.rem(mine // 2, 2)
+    layer_at = mine // 4
+    for number, ref in enumerate((near, across, far, far_across)):
+        owner_core = core if number < 2 else 1 - core
+        owner_row = row if number % 2 == 0 else 1 - row
+        for back in range(4):
+            owner_layer = lax.rem(layer_at + 4 - back, 4)
+            piece = owner_core * CHIPS + owner_layer * 2 + owner_row
+            rows = ref[pl.ds(back * ROWS, ROWS)].astype(F32) * inverse
+            flat[pl.ds(pl.multiple_of(piece * ROWS, 8), ROWS)] = rows
+    q_out[...] = flat[: HEADS * HD]
+    k_out[...] = flat[HEADS * HD :]
 
 
 def pack_kernel(keys, values, out, both, sems):
@@ -414,10 +413,10 @@
             pltpu.VMEM((2, wide, 2 * HD), BF16),
             pltpu.VMEM((2, 2 * HD, wide), F32),
             pltpu.VMEM((SLOTS, BLK, 2 * HD), BF16),
-            pltpu.VMEM((HD, pair), BF16),
+            pltpu.VMEM((STEPS, HD, pair), BF16),
             pltpu.VMEM((STEPS, HD, pair), BF16),
             pltpu.VMEM((STEPS, pair, 2 * HD), F32),
-            pltpu.VMEM((pair, 2 * HD), BF16),
+            pltpu.VMEM((STEPS, pair, 2 * HD), BF16),
             pltpu.VMEM((STEPS, 2 * HD, pair), BF16),
             pltpu.VMEM((2, chunks, HD, pair), F32),
             pltpu.VMEM((2, chunks, HD, pair), F32),
@@ -430,14 +429,12 @@
             pltpu.VMEM((HD, HD), F32),
             pltpu.VMEM(((HEADS + 1) * HD, HD), F32),
             pltpu.VMEM((8, BLK), F32),
-            pltpu.VMEM((pair, wide), F32),
-            pltpu.VMEM((pair, wide), F32),
-            pltpu.VMEM((pair, wide), BF16),
-            pltpu.VMEM((pair, wide), BF16),
-            pltpu.VMEM((pair, 2 * HD), F32),
-            pltpu.VMEM((pair, 2 * HD), BF16),
-            pltpu.VMEM((HD, pair), BF16),
-            pltpu.VMEM((chunks, 1, pair), F32),
+            pltpu.VMEM((2, pair, wide), F32),
+            pltpu.VMEM((2, pair, wide), F32),
+            pltpu.VMEM((2, pair, wide), BF16),
+            pltpu.VMEM((2, pair, wide), BF16),
+            pltpu.VMEM((2, pair, 2 * HD), F32),
+            pltpu.VMEM((2, chunks, 1, pair), F32),
         ],
         compiler_params=pltpu.CompilerParams(vmem_limit_bytes=ATTEND_VMEM),
         name="attend",
@@ -479,34 +476,31 @@
     near, far = attend(info, same, other, k_map[0], early, late, q_map_t)
     met = (near + lax.ppermute(far, "seq", OTHER_CORE).astype(F32)).astype(BF16)
     pieces = lax.all_to_all(met, "seq", 0, 0, axis_index_groups=SAME_CORE, tiled=True)
+    everyone = SEQ * KV
     chunk, stats = pl.pallas_call(
         fold_kernel,
-        out_shape=(shape((ROWS, BLK), BF16), shape((KV, 8, BLK), F32)),
+        out_shape=(shape((ROWS, BLK), BF16), shape((everyone, 1, BLK), F32)),
         in_specs=[vmem()],
         out_specs=(vmem(), vmem()),
         compiler_params=small,
         name="fold",
     )(pieces)
-    stats = lax.all_to_all(stats, "kv", 0, 0, tiled=True)
-    payload, loss = pl.pallas_call(
-        share_kernel,
-        out_shape=(shape((CHIPS, PAYLOAD, BLK), BF16), shape((8, BLK), F32)),
-        in_specs=[vmem(), vmem()],
-        out_specs=(vmem(), vmem()),
-        compiler_params=small,
-        name="share",
-    )(chunk, stats)
-    own = lax.all_to_all(payload, "seq", 0, 0, axis_index_groups=SAME_CORE, tiled=True)
-    sibling = lax.ppermute(own, "seq", OTHER_CORE)
-    grad_q, grad_k = pl.pallas_call(
+    stats = lax.all_to_all(stats, ("seq", "kv"), 0, 0, tiled=True)
+    column = [chunk] + [lax.ppermute(chunk, "seq", route) for route in LAYER_SHIFTS]
+    near = jnp.concatenate(column, axis=0)
+    across = lax.ppermute(near, "seq", OTHER_ROW)
+    far = lax.ppermute(near, "seq", OTHER_CORE)
+    far_across = lax.ppermute(across, "seq", OTHER_CORE)
+    grad_q, grad_k, loss = pl.pallas_call(
         scale_kernel,
-        out_shape=(shape((HEADS * HD, HD), F32), shape((HD, HD), F32)),
-        in_specs=[smem(), vmem(), vmem()],
-        out_specs=(vmem(), vmem()),
+        out_shape=(shape((HEADS * HD, HD), F32), shape((HD, HD), F32), shape((1, 1), F32)),
+        in_specs=[smem()] + [vmem()] * 5,
+        out_specs=(vmem(), vmem(), vmem()),
+        scratch_shapes=[pltpu.VMEM(((HEADS + 1) * HD, HD), F32)],
         compiler_params=small,
         name="scale",
-    )(place, own, sibling)
-    return grad_q.reshape(HEADS, HD, HD), grad_k.reshape(1, HD, HD), loss[0, 0]
+    )(place, stats, near, across, far, far_across)
+    return grad_q.reshape(HEADS, HD, HD), grad_k.reshape(1, HD, HD), loss.reshape(())
 
 
 def solution(mesh):

time: 91.3 us -> 92 us (level)
  waiting for transfers between devices: 5.31 us -> 12.6 us
  blocking collectives: 55.3 us -> 49 us
  starting transfers between devices: 2.27 us -> 6.02 us
  Pallas kernels: 25.1 us -> 22 us
    ppermute x1 -> x6, waiting for transfers between devices: 0.88 us -> 8.15 us  [the longest x3 4.79 us: layer(): lax.ppermute(chunk, 'seq', route)]
    all_to_all x2 -> x1, blocking collectives: 23.4 us -> 17 us  [layer(): stats = lax.all_to_all(stats, ('seq', 'kv'), 0, 0, tiled=True)]
    ppermute x1 -> x6, starting transfers between devices: 0.01 us -> 3.75 us  [the longest x3 2.67 us: layer(): lax.ppermute(chunk, 'seq', route)]
    pallas_call x1, Pallas kernels: 17.6 us -> 14.3 us  [attend(): pl.pallas_call(main_kernel, out_shape=(shape((CHIPS, PAYLOAD, BLK), F32),...]
  transfers between devices with their start and end apart: 4 -> 9, of which waited for: 3 -> 4; matrix products, arithmetic and copies ran while one was open for 1% -> 1% of each run, Pallas kernels for 5% -> 5%
where the time goes in v3:
time: 92 us; the launch traced here: 91 us
  blocking collectives  49 us (53%)
  Pallas kernels  22 us (24%)
  waiting for transfers between devices  12.6 us (14%)
  starting transfers between devices  6.02 us (7%)
    all_to_all x1, blocking collectives, layer(): lax.all_to_all(sent, 'seq', 0, 0, axis_index_groups=SAME_CORE, tiled=True)  22.4 us
    all_to_all x1, blocking collectives, layer(): stats = lax.all_to_all(stats, ('seq', 'kv'), 0, 0, tiled=True)  17 us
    pallas_call x1, Pallas kernels, attend(): pl.pallas_call(main_kernel, out_shape=(shape((CHIPS, PAYLOAD, BLK), F32),...  14.3 us
    all_to_all x1, blocking collectives, layer(): lax.all_to_all(met, 'seq', 0, 0, axis_index_groups=SAME_CORE, tiled=True)  9.5 us
    ppermute x3, waiting for transfers between devices, layer(): lax.ppermute(chunk, 'seq', route)  4.79 us
    pallas_call x1, Pallas kernels, layer(): pl.pallas_call(list_kernel, out_shape=shape((128,), jnp.int32), in_specs=...  4.48 us
    ppermute x1, waiting for transfers between devices, layer(): late = lax.ppermute(late, 'seq', MIRROR)  3.4 us
    ppermute x1, waiting for transfers between devices, layer(): across = lax.ppermute(near, 'seq', OTHER_ROW)  3.35 us
  transfers between devices with their start and end apart: 9, of which 4 were waited for; matrix products, arithmetic and copies ran while one was open for 1% of the time, Pallas kernels for 5%

profile of v3, /device:TPU:0, one launch (start us, length us, event | category | flops | bytes accessed | tf_op | source)
XLA Modules:
  0.0 91.0 jit_solution(4346084332161146318)
XLA Ops:
  0.6 1.9 %pack.1 = bf16[8,256,256]{2,1,0:T(8,128)(2,1)} custom-call(bf16[256,128]{1,0:T(8,128)(2,1)} %bitcast.18, bf16[256,128]{1,0:T(8,128)(2,1)} %bitcast.19), custom_call_target="tpu_custom_call" | custom-call | tf_op jit(solution)/shard_map/pack/pallas_call | solution.py:446
  2.6 0.0 copy-start.1
  2.6 22.4 %all_to_all.15.same = bf16[8,256,256]{2,1,0:T(8,128)(2,1)S(1)} all-to-all(bf16[8,256,256]{2,1,0:T(8,128)(2,1)} %pack.1), channel_id=1, replica_groups={{0,16,32,48,64,80,96,112},{8,24,40,56,72,88,104,120},{1,17,33,49,65,81,..., dimensions={0} | all-to-all | bytes 2097152 | tf_op jit(solution)/shard_map/all_to_all | solution.py:458
  25.0 0.0 collective-permute-start
  25.0 0.0 copy-start.3
  25.1 0.0 copy-start.2
  25.1 1.7 %collective-permute-start.1 = (bf16[8,128,128]{2,1,0:T(8,128)(2,1)S(1)}, bf16[8,128,128]{2,1,0:T(8,128)(2,1)S(1)}, u32[]{:S(2)}, u32[]{:S(2)}) collective-permute-start(bf16[8,128,128]{2,1,0:T(8,128)(2,1)S(1)} %bitcast.17), channel_id=1, source_target_pairs={{0,120},{8,112},{16,104},{24,96},{32,88},{40,80},{48,72},{56,64},{... | collective-permute-start | bytes 786440 | tf_op jit(solution)/shard_map/ppermute | solution.py:463
  26.8 0.1 copy.12
  26.9 0.1 reshape.22.pairs
  27.1 0.2 copy.15
  27.3 0.0 copy-start
  27.3 4.5 %list.1.info = s32[128]{0:T(128)S(1)} custom-call(s32[1]{0:T(128)} %bitcast.place, s32[544]{0:T(1024)S(1)} %reshape.22.pairs), custom_call_target="tpu_custom_call" | custom-call | flops 5000000000 | bytes 100000 | tf_op jit(solution)/shard_map/list/pallas_call | solution.py:465
  31.8 3.4 %collective-permute-done.1.late = bf16[8,128,128]{2,1,0:T(8,128)(2,1)S(1)} collective-permute-done((bf16[8,128,128]{2,1,0:T(8,128)(2,1)S(1)}, bf16[8,128,128]{2,1,0:T(8,128)(2,1)S(1)}, u32[]{:S(2)}, u32[]{:S(2)}) %collective-permute-start.1) | collective-permute-done | bytes 262176 | tf_op jit(solution)/shard_map/ppermute | solution.py:463
  35.2 0.0 collective-permute-done.other
  35.2 14.3 %attend.1 = (f32[8,80,128]{2,1,0:T(8,128)S(1)}, bf16[8,80,128]{2,1,0:T(8,128)(2,1)S(1)}) custom-call(s32[128]{0:T(128)S(1)} %list.1.info, bf16[8,256,256]{2,1,0:T(8,128)(2,1)S(1)} %all_to_all.15.same, bf16[8,256,256]{2,1,0:T(8,128)(2,1)S(1)} %collective-permute-done.other, bf16[128,128]{1,0:T(8,128)(2,1)S(1)} %bitcast.16, bf16[8,128,128]{2,1,0:T(8,128)(2,1)S(1)} %bitcast.15, ...), custom_call_target="tpu_custom_call" | custom-call | tf_op jit(solution)/shard_map/attend/pallas_call | solution.py:405
  49.5 0.6 collective-permute-start.2
  50.1 1.0 %collective-permute-done.2 = bf16[8,80,128]{2,1,0:T(8,128)(2,1)S(1)} collective-permute-done((bf16[8,80,128]{2,1,0:T(8,128)(2,1)S(1)}, bf16[8,80,128]{2,1,0:T(8,128)(2,1)S(1)}, u32[]{:S(2)}, u32[]{:S(2)}) %collective-permute-start.2) | collective-permute-done | bytes 163872 | tf_op jit(solution)/shard_map/ppermute | solution.py:477
  51.2 9.5 %all_to_all.16.pieces = bf16[8,80,128]{2,1,0:T(8,128)(2,1)S(1)} all-to-all(bf16[8,80,128]{2,1,0:T(8,128)(2,1)S(1)} %add_convert_fusion), channel_id=1, replica_groups={{0,16,32,48,64,80,96,112},{8,24,40,56,72,88,104,120},{1,17,33,49,65,81,..., dimensions={0} | all-to-all | bytes 327680 | tf_op jit(solution)/shard_map/all_to_all | solution.py:478
  60.7 0.2 fold.1
  60.8 1.0 %collective-permute-start.5 = (bf16[72,128]{1,0:T(8,128)(2,1)S(1)}, bf16[72,128]{1,0:T(8,128)(2,1)S(1)}, u32[]{:S(2)}, u32[]{:S(2)}) collective-permute-start(bf16[72,128]{1,0:T(8,128)(2,1)S(1)} %get-tuple-element.13), channel_id=1, source_target_pairs={{0,96},{8,104},{16,112},{24,120},{32,0},{40,8},{48,16},{56,24},{64... | collective-permute-start | bytes 55304 | tf_op jit(solution)/shard_map/ppermute | solution.py:489
  61.9 1.5 %collective-permute-start.4 = (bf16[72,128]{1,0:T(8,128)(2,1)S(1)}, bf16[72,128]{1,0:T(8,128)(2,1)S(1)}, u32[]{:S(2)}, u32[]{:S(2)}) collective-permute-start(bf16[72,128]{1,0:T(8,128)(2,1)S(1)} %get-tuple-element.13), channel_id=1, source_target_pairs={{0,64},{8,72},{16,80},{24,88},{32,96},{40,104},{48,112},{56,120},{... | collective-permute-start | bytes 55304 | tf_op jit(solution)/shard_map/ppermute | solution.py:489
  63.3 0.2 collective-permute-start.3
  63.5 4.8 %collective-permute-done.3 = bf16[72,128]{1,0:T(8,128)(2,1)S(1)} collective-permute-done((bf16[72,128]{1,0:T(8,128)(2,1)S(1)}, bf16[72,128]{1,0:T(8,128)(2,1)S(1)}, u32[]{:S(2)}, u32[]{:S(2)}) %collective-permute-start.3) | collective-permute-done | bytes 18464 | tf_op jit(solution)/shard_map/ppermute | solution.py:489
  68.3 0.0 collective-permute-done.4
  68.3 0.0 collective-permute-done.5
  68.4 1.1 %collective-permute-start.6 = (bf16[288,128]{1,0:T(8,128)(2,1)S(1)}, bf16[288,128]{1,0:T(8,128)(2,1)S(1)}, u32[]{:S(2)}, u32[]{:S(2)}) collective-permute-start(bf16[288,128]{1,0:T(8,128)(2,1)S(1)} %constant_dynamic-update-slice_fusion.near), channel_id=1, source_target_pairs={{0,16},{8,24},{16,0},{24,8},{32,48},{40,56},{48,32},{56,40},{64,80... | collective-permute-start | bytes 221192 | tf_op jit(solution)/shard_map/ppermute | solution.py:491
  69.4 0.0 collective-permute-start.7
  69.4 3.4 %collective-permute-done.6.across = bf16[288,128]{1,0:T(8,128)(2,1)S(1)} collective-permute-done((bf16[288,128]{1,0:T(8,128)(2,1)S(1)}, bf16[288,128]{1,0:T(8,128)(2,1)S(1)}, u32[]{:S(2)}, u32[]{:S(2)}) %collective-permute-start.6) | collective-permute-done | bytes 73760 | tf_op jit(solution)/shard_map/ppermute | solution.py:491
  72.8 17.0 %all_to_all.17.stats = f32[128,1,128]{2,1,0:T(1,128)S(1)} all-to-all(f32[128,1,128]{2,1,0:T(1,128)S(1)} %get-tuple-element.12), channel_id=1, replica_groups=mesh['seq'=16,'kv'=8] {'seq','kv'}, dimensions={0} | all-to-all | bytes 131072 | tf_op jit(solution)/shard_map/all_to_all | solution.py:488
  89.8 0.0 collective-permute-done.7.far
  89.8 0.0 collective-permute-done.8.far_across
  89.8 1.1 %scale.1 = (f32[1024,128]{1,0:T(8,128)}, f32[128,128]{1,0:T(8,128)}, f32[1,1]{1,0:T(1,128)}) custom-call(s32[1]{0:T(128)} %bitcast.place, f32[128,1,128]{2,1,0:T(1,128)S(1)} %all_to_all.17.stats, bf16[288,128]{1,0:T(8,128)(2,1)S(1)} %constant_dynamic-update-slice_fusion.near, bf16[288,128]{1,0:T(8,128)(2,1)S(1)} %collective-permute-done.6.across, ...), custom_call_target="tpu_custom_call" | custom-call | tf_op jit(solution)/shard_map/scale/pallas_call | solution.py:494
  (13 shorter events, 0.2 us)
Async XLA Ops:
  2.6 22.4 %copy-start.1 = (bf16[256,8,128]{2,1,0:T(8,128)(2,1)S(1)}, bf16[256,8,128]{2,1,0:T(8,128)(2,1)}, u32[]{:S(2)}) copy-start(bf16[256,8,128]{2,1,0:T(8,128)(2,1)} %param.6) | copy-start | bytes 1572868
  25.0 10.2 %collective-permute-start = (bf16[8,256,256]{2,1,0:T(8,128)(2,1)S(1)}, bf16[8,256,256]{2,1,0:T(8,128)(2,1)S(1)}, u32[]{:S(2)}, u32[]{:S(2)}) collective-permute-start(bf16[8,256,256]{2,1,0:T(8,128)(2,1)S(1)} %all_to_all.15.same), channel_id=1, source_target_pairs={{0,8},{8,0},{16,24},{24,16},{32,40},{40,32},{48,56},{56,48},{64,72... | collective-permute-start | bytes 3145736 | tf_op jit(solution)/shard_map/ppermute | solution.py:459
  25.0 1.7 %copy-start.3 = (s32[272,2]{0,1:T(2,128)S(1)}, s32[272,2]{0,1:T(2,128)}, u32[]{:S(2)}) copy-start(s32[272,2]{0,1:T(2,128)} %param.11) | copy-start | bytes 6532
  25.1 2.0 %copy-start.2 = (bf16[8,128,128]{2,1,0:T(8,128)(2,1)S(1)}, bf16[8,128,128]{2,1,0:T(8,128)(2,1)}, u32[]{:S(2)}) copy-start(bf16[8,128,128]{2,1,0:T(8,128)(2,1)} %param.9) | copy-start | bytes 786436
  25.1 10.1 %collective-permute-start.1 = (bf16[8,128,128]{2,1,0:T(8,128)(2,1)S(1)}, bf16[8,128,128]{2,1,0:T(8,128)(2,1)S(1)}, u32[]{:S(2)}, u32[]{:S(2)}) collective-permute-start(bf16[8,128,128]{2,1,0:T(8,128)(2,1)S(1)} %bitcast.17), channel_id=1, source_target_pairs={{0,120},{8,112},{16,104},{24,96},{32,88},{40,80},{48,72},{56,64},{... | collective-permute-start | bytes 786440 | tf_op jit(solution)/shard_map/ppermute | solution.py:463
  27.3 7.9 %copy-start = (bf16[1,128,128]{2,1,0:T(8,128)(2,1)S(1)}, bf16[1,128,128]{2,1,0:T(8,128)(2,1)}, u32[]{:S(2)}) copy-start(bf16[1,128,128]{2,1,0:T(8,128)(2,1)} %param.10) | copy-start | bytes 98308
  49.5 1.6 %collective-permute-start.2 = (bf16[8,80,128]{2,1,0:T(8,128)(2,1)S(1)}, bf16[8,80,128]{2,1,0:T(8,128)(2,1)S(1)}, u32[]{:S(2)}, u32[]{:S(2)}) collective-permute-start(bf16[8,80,128]{2,1,0:T(8,128)(2,1)S(1)} %get-tuple-element.11), channel_id=1, source_target_pairs={{0,8},{8,0},{16,24},{24,16},{32,40},{40,32},{48,56},{56,48},{64,72... | collective-permute-start | bytes 491528 | tf_op jit(solution)/shard_map/ppermute | solution.py:477
  60.8 7.5 %collective-permute-start.5 = (bf16[72,128]{1,0:T(8,128)(2,1)S(1)}, bf16[72,128]{1,0:T(8,128)(2,1)S(1)}, u32[]{:S(2)}, u32[]{:S(2)}) collective-permute-start(bf16[72,128]{1,0:T(8,128)(2,1)S(1)} %get-tuple-element.13), channel_id=1, source_target_pairs={{0,96},{8,104},{16,112},{24,120},{32,0},{40,8},{48,16},{56,24},{64... | collective-permute-start | bytes 55304 | tf_op jit(solution)/shard_map/ppermute | solution.py:489
  61.9 6.5 %collective-permute-start.4 = (bf16[72,128]{1,0:T(8,128)(2,1)S(1)}, bf16[72,128]{1,0:T(8,128)(2,1)S(1)}, u32[]{:S(2)}, u32[]{:S(2)}) collective-permute-start(bf16[72,128]{1,0:T(8,128)(2,1)S(1)} %get-tuple-element.13), channel_id=1, source_target_pairs={{0,64},{8,72},{16,80},{24,88},{32,96},{40,104},{48,112},{56,120},{... | collective-permute-start | bytes 55304 | tf_op jit(solution)/shard_map/ppermute | solution.py:489
  63.3 5.0 %collective-permute-start.3 = (bf16[72,128]{1,0:T(8,128)(2,1)S(1)}, bf16[72,128]{1,0:T(8,128)(2,1)S(1)}, u32[]{:S(2)}, u32[]{:S(2)}) collective-permute-start(bf16[72,128]{1,0:T(8,128)(2,1)S(1)} %get-tuple-element.13), channel_id=1, source_target_pairs={{0,32},{8,40},{16,48},{24,56},{32,64},{40,72},{48,80},{56,88},{64,... | collective-permute-start | bytes 55304 | tf_op jit(solution)/shard_map/ppermute | solution.py:489
  68.4 4.4 %collective-permute-start.6 = (bf16[288,128]{1,0:T(8,128)(2,1)S(1)}, bf16[288,128]{1,0:T(8,128)(2,1)S(1)}, u32[]{:S(2)}, u32[]{:S(2)}) collective-permute-start(bf16[288,128]{1,0:T(8,128)(2,1)S(1)} %constant_dynamic-update-slice_fusion.near), channel_id=1, source_target_pairs={{0,16},{8,24},{16,0},{24,8},{32,48},{40,56},{48,32},{56,40},{64,80... | collective-permute-start | bytes 221192 | tf_op jit(solution)/shard_map/ppermute | solution.py:491
  69.4 20.4 %collective-permute-start.7 = (bf16[288,128]{1,0:T(8,128)(2,1)S(1)}, bf16[288,128]{1,0:T(8,128)(2,1)S(1)}, u32[]{:S(2)}, u32[]{:S(2)}) collective-permute-start(bf16[288,128]{1,0:T(8,128)(2,1)S(1)} %constant_dynamic-update-slice_fusion.near), channel_id=1, source_target_pairs={{0,8},{8,0},{16,24},{24,16},{32,40},{40,32},{48,56},{56,48},{64,72... | collective-permute-start | bytes 221192 | tf_op jit(solution)/shard_map/ppermute | solution.py:492
  72.8 17.1 %collective-permute-start.8 = (bf16[288,128]{1,0:T(8,128)(2,1)S(1)}, bf16[288,128]{1,0:T(8,128)(2,1)S(1)}, u32[]{:S(2)}, u32[]{:S(2)}) collective-permute-start(bf16[288,128]{1,0:T(8,128)(2,1)S(1)} %collective-permute-done.6.across), channel_id=1, source_target_pairs={{0,8},{8,0},{16,24},{24,16},{32,40},{40,32},{48,56},{56,48},{64,72... | collective-permute-start | bytes 221192 | tf_op jit(solution)/shard_map/ppermute | solution.py:493

commit v4 on v3

--- a/solution.py
+++ b/solution.py
@@ -344,7 +344,7 @@
     stats[...] = jnp.broadcast_to(row[None], stats.shape)
 
 
-def scale_kernel(place, stats, near, across, far, far_across, q_out, k_out, loss, flat):
+def scale_kernel(place, stats, layer0, layer1, layer2, layer3, q_out, k_out, loss, flat):
     total = jnp.sum(stats[...], axis=0)
     left = lax.broadcasted_iota(jnp.int32, (1, BLK), 1) < BLK // 2
     squared = jnp.sum(jnp.where(left, total, 0.0), axis=1, keepdims=True)
@@ -356,13 +356,13 @@
     core = lax.rem(mine, 2)
     row = lax.rem(mine // 2, 2)
     layer_at = mine // 4
-    for number, ref in enumerate((near, across, far, far_across)):
-        owner_core = core if number < 2 else 1 - core
-        owner_row = row if number % 2 == 0 else 1 - row
-        for back in range(4):
-            owner_layer = lax.rem(layer_at + 4 - back, 4)
+    for back, ref in enumerate((layer0, layer1, layer2, layer3)):
+        owner_layer = lax.rem(layer_at + 4 - back, 4)
+        for number in range(4):
+            owner_core = core if number < 2 else 1 - core
+            owner_row = row if number % 2 == 0 else 1 - row
             piece = owner_core * CHIPS + owner_layer * 2 + owner_row
-            rows = ref[pl.ds(back * ROWS, ROWS)].astype(F32) * inverse
+            rows = ref[pl.ds(number * ROWS, ROWS)].astype(F32) * inverse
             flat[pl.ds(pl.multiple_of(piece * ROWS, 8), ROWS)] = rows
     q_out[...] = flat[: HEADS * HD]
     k_out[...] = flat[HEADS * HD :]
@@ -486,11 +486,11 @@
         name="fold",
     )(pieces)
     stats = lax.all_to_all(stats, ("seq", "kv"), 0, 0, tiled=True)
-    column = [chunk] + [lax.ppermute(chunk, "seq", route) for route in LAYER_SHIFTS]
-    near = jnp.concatenate(column, axis=0)
-    across = lax.ppermute(near, "seq", OTHER_ROW)
-    far = lax.ppermute(near, "seq", OTHER_CORE)
-    far_across = lax.ppermute(across, "seq", OTHER_CORE)
+    across = lax.ppermute(chunk, "seq", OTHER_ROW)
+    aside = lax.ppermute(chunk, "seq", OTHER_CORE)
+    diagonal = lax.ppermute(across, "seq", OTHER_CORE)
+    near = jnp.concatenate([chunk, across, aside, diagonal], axis=0)
+    layers = [near] + [lax.ppermute(near, "seq", route) for route in LAYER_SHIFTS]
     grad_q, grad_k, loss = pl.pallas_call(
         scale_kernel,
         out_shape=(shape((HEADS * HD, HD), F32), shape((HD, HD), F32), shape((1, 1), F32)),
@@ -499,7 +499,7 @@
         scratch_shapes=[pltpu.VMEM(((HEADS + 1) * HD, HD), F32)],
         compiler_params=small,
         name="scale",
-    )(place, stats, near, across, far, far_across)
+    )(place, stats, *layers)
     return grad_q.reshape(HEADS, HD, HD), grad_k.reshape(1, HD, HD), loss.reshape(())
 
 

time: 92 us -> 90.2 us (0.980)
  waiting for transfers between devices: 12.6 us -> 8.57 us
  blocking collectives: 49 us -> 51.3 us
    ppermute x6, waiting for transfers between devices: 8.15 us -> 4.13 us  [the longest x1 2.97 us: layer(): across = lax.ppermute(chunk, 'seq', OTHER_ROW)]
    all_to_all x1, blocking collectives: 17 us -> 19.4 us  [layer(): stats = lax.all_to_all(stats, ('seq', 'kv'), 0, 0, tiled=True)]
where the time goes in v4:
time: 90.2 us; the launch traced here: 89.1 us
  blocking collectives  51.3 us (57%)
  Pallas kernels  22 us (24%)
  waiting for transfers between devices  8.57 us (10%)
  starting transfers between devices  5.82 us (6%)
    all_to_all x1, blocking collectives, layer(): lax.all_to_all(sent, 'seq', 0, 0, axis_index_groups=SAME_CORE, tiled=True)  22.4 us
    all_to_all x1, blocking collectives, layer(): stats = lax.all_to_all(stats, ('seq', 'kv'), 0, 0, tiled=True)  19.4 us
    pallas_call x1, Pallas kernels, attend(): pl.pallas_call(main_kernel, out_shape=(shape((CHIPS, PAYLOAD, BLK), F32),...  14.3 us
    all_to_all x1, blocking collectives, layer(): lax.all_to_all(met, 'seq', 0, 0, axis_index_groups=SAME_CORE, tiled=True)  9.5 us
    pallas_call x1, Pallas kernels, layer(): pl.pallas_call(list_kernel, out_shape=shape((128,), jnp.int32), in_specs=...  4.48 us
    ppermute x1, waiting for transfers between devices, layer(): late = lax.ppermute(late, 'seq', MIRROR)  3.4 us
    ppermute x1, waiting for transfers between devices, layer(): across = lax.ppermute(chunk, 'seq', OTHER_ROW)  2.97 us
    ppermute x3, starting transfers between devices, layer(): lax.ppermute(near, 'seq', route)  2.6 us
  transfers between devices with their start and end apart: 9, of which 4 were waited for; matrix products, arithmetic and copies ran while one was open for 1% of the time, Pallas kernels for 5%

profile of v4, /device:TPU:0, one launch (start us, length us, event | category | flops | bytes accessed | tf_op | source)
XLA Modules:
  0.0 89.1 jit_solution(12877882629404643396)
XLA Ops:
  0.6 1.9 %pack.1 = bf16[8,256,256]{2,1,0:T(8,128)(2,1)} custom-call(bf16[256,128]{1,0:T(8,128)(2,1)} %bitcast.18, bf16[256,128]{1,0:T(8,128)(2,1)} %bitcast.19), custom_call_target="tpu_custom_call" | custom-call | tf_op jit(solution)/shard_map/pack/pallas_call | solution.py:446
  2.6 0.0 copy-start.1
  2.6 22.4 %all_to_all.15.same = bf16[8,256,256]{2,1,0:T(8,128)(2,1)S(1)} all-to-all(bf16[8,256,256]{2,1,0:T(8,128)(2,1)} %pack.1), channel_id=1, replica_groups={{0,16,32,48,64,80,96,112},{8,24,40,56,72,88,104,120},{1,17,33,49,65,81,..., dimensions={0} | all-to-all | bytes 2097152 | tf_op jit(solution)/shard_map/all_to_all | solution.py:458
  25.0 0.0 collective-permute-start
  25.0 0.0 copy-start.3
  25.1 0.0 copy-start.2
  25.1 1.7 %collective-permute-start.1 = (bf16[8,128,128]{2,1,0:T(8,128)(2,1)S(1)}, bf16[8,128,128]{2,1,0:T(8,128)(2,1)S(1)}, u32[]{:S(2)}, u32[]{:S(2)}) collective-permute-start(bf16[8,128,128]{2,1,0:T(8,128)(2,1)S(1)} %bitcast.17), channel_id=1, source_target_pairs={{0,120},{8,112},{16,104},{24,96},{32,88},{40,80},{48,72},{56,64},{... | collective-permute-start | bytes 786440 | tf_op jit(solution)/shard_map/ppermute | solution.py:463
  26.8 0.1 copy.12
  26.9 0.1 reshape.22.pairs
  27.1 0.2 copy.15
  27.3 0.0 copy-start
  27.3 4.5 %list.1.info = s32[128]{0:T(128)S(1)} custom-call(s32[1]{0:T(128)} %bitcast.place, s32[544]{0:T(1024)S(1)} %reshape.22.pairs), custom_call_target="tpu_custom_call" | custom-call | flops 5000000000 | bytes 100000 | tf_op jit(solution)/shard_map/list/pallas_call | solution.py:465
  31.8 3.4 %collective-permute-done.1.late = bf16[8,128,128]{2,1,0:T(8,128)(2,1)S(1)} collective-permute-done((bf16[8,128,128]{2,1,0:T(8,128)(2,1)S(1)}, bf16[8,128,128]{2,1,0:T(8,128)(2,1)S(1)}, u32[]{:S(2)}, u32[]{:S(2)}) %collective-permute-start.1) | collective-permute-done | bytes 262176 | tf_op jit(solution)/shard_map/ppermute | solution.py:463
  35.2 0.0 collective-permute-done.other
  35.2 14.3 %attend.1 = (f32[8,80,128]{2,1,0:T(8,128)S(1)}, bf16[8,80,128]{2,1,0:T(8,128)(2,1)S(1)}) custom-call(s32[128]{0:T(128)S(1)} %list.1.info, bf16[8,256,256]{2,1,0:T(8,128)(2,1)S(1)} %all_to_all.15.same, bf16[8,256,256]{2,1,0:T(8,128)(2,1)S(1)} %collective-permute-done.other, bf16[128,128]{1,0:T(8,128)(2,1)S(1)} %bitcast.16, bf16[8,128,128]{2,1,0:T(8,128)(2,1)S(1)} %bitcast.15, ...), custom_call_target="tpu_custom_call" | custom-call | tf_op jit(solution)/shard_map/attend/pallas_call | solution.py:405
  49.5 0.6 collective-permute-start.2
  50.1 1.0 %collective-permute-done.2 = bf16[8,80,128]{2,1,0:T(8,128)(2,1)S(1)} collective-permute-done((bf16[8,80,128]{2,1,0:T(8,128)(2,1)S(1)}, bf16[8,80,128]{2,1,0:T(8,128)(2,1)S(1)}, u32[]{:S(2)}, u32[]{:S(2)}) %collective-permute-start.2) | collective-permute-done | bytes 163872 | tf_op jit(solution)/shard_map/ppermute | solution.py:477
  51.2 9.5 %all_to_all.16.pieces = bf16[8,80,128]{2,1,0:T(8,128)(2,1)S(1)} all-to-all(bf16[8,80,128]{2,1,0:T(8,128)(2,1)S(1)} %add_convert_fusion), channel_id=1, replica_groups={{0,16,32,48,64,80,96,112},{8,24,40,56,72,88,104,120},{1,17,33,49,65,81,..., dimensions={0} | all-to-all | bytes 327680 | tf_op jit(solution)/shard_map/all_to_all | solution.py:478
  60.7 0.2 fold.1
  60.8 0.1 collective-permute-start.4
  60.9 0.9 collective-permute-start.3
  61.8 3.0 %collective-permute-done.3 = bf16[72,128]{1,0:T(8,128)(2,1)S(1)} collective-permute-done((bf16[72,128]{1,0:T(8,128)(2,1)S(1)}, bf16[72,128]{1,0:T(8,128)(2,1)S(1)}, u32[]{:S(2)}, u32[]{:S(2)}) %collective-permute-start.3) | collective-permute-done | bytes 18464 | tf_op jit(solution)/shard_map/ppermute | solution.py:489
  64.8 0.0 collective-permute-done.4
  64.8 1.2 %collective-permute-done.5 = bf16[72,128]{1,0:T(8,128)(2,1)S(1)} collective-permute-done((bf16[72,128]{1,0:T(8,128)(2,1)S(1)}, bf16[72,128]{1,0:T(8,128)(2,1)S(1)}, u32[]{:S(2)}, u32[]{:S(2)}) %collective-permute-start.5) | collective-permute-done | bytes 18464 | tf_op jit(solution)/shard_map/ppermute | solution.py:491
  66.0 0.9 %collective-permute-start.8 = (bf16[288,128]{1,0:T(8,128)(2,1)S(1)}, bf16[288,128]{1,0:T(8,128)(2,1)S(1)}, u32[]{:S(2)}, u32[]{:S(2)}) collective-permute-start(bf16[288,128]{1,0:T(8,128)(2,1)S(1)} %constant_dynamic-update-slice_fusion.layer0), channel_id=1, source_target_pairs={{0,96},{8,104},{16,112},{24,120},{32,0},{40,8},{48,16},{56,24},{64... | collective-permute-start | bytes 221192 | tf_op jit(solution)/shard_map/ppermute | solution.py:493
  66.9 1.5 %collective-permute-start.7 = (bf16[288,128]{1,0:T(8,128)(2,1)S(1)}, bf16[288,128]{1,0:T(8,128)(2,1)S(1)}, u32[]{:S(2)}, u32[]{:S(2)}) collective-permute-start(bf16[288,128]{1,0:T(8,128)(2,1)S(1)} %constant_dynamic-update-slice_fusion.layer0), channel_id=1, source_target_pairs={{0,64},{8,72},{16,80},{24,88},{32,96},{40,104},{48,112},{56,120},{... | collective-permute-start | bytes 221192 | tf_op jit(solution)/shard_map/ppermute | solution.py:493
  68.4 0.2 collective-permute-start.6
  68.6 19.4 %all_to_all.17.stats = f32[128,1,128]{2,1,0:T(1,128)S(1)} all-to-all(f32[128,1,128]{2,1,0:T(1,128)S(1)} %get-tuple-element.12), channel_id=1, replica_groups=mesh['seq'=16,'kv'=8] {'seq','kv'}, dimensions={0} | all-to-all | bytes 131072 | tf_op jit(solution)/shard_map/all_to_all | solution.py:488
  88.0 0.0 collective-permute-done.8.layer3
  88.0 0.0 collective-permute-done.7.layer2
  88.0 0.0 collective-permute-done.6.layer1
  88.0 1.1 %scale.1 = (f32[1024,128]{1,0:T(8,128)}, f32[128,128]{1,0:T(8,128)}, f32[1,1]{1,0:T(1,128)}) custom-call(s32[1]{0:T(128)} %bitcast.place, f32[128,1,128]{2,1,0:T(1,128)S(1)} %all_to_all.17.stats, bf16[288,128]{1,0:T(8,128)(2,1)S(1)} %constant_dynamic-update-slice_fusion.layer0, bf16[288,128]{1,0:T(8,128)(2,1)S(1)} %collective-permute-done.6.layer1, ...), custom_call_target="tpu_custom_call" | custom-call | tf_op jit(solution)/shard_map/scale/pallas_call | solution.py:494
  (13 shorter events, 0.2 us)
Async XLA Ops:
  2.6 22.4 %copy-start.1 = (bf16[256,8,128]{2,1,0:T(8,128)(2,1)S(1)}, bf16[256,8,128]{2,1,0:T(8,128)(2,1)}, u32[]{:S(2)}) copy-start(bf16[256,8,128]{2,1,0:T(8,128)(2,1)} %param.6) | copy-start | bytes 1572868
  25.0 10.2 %collective-permute-start = (bf16[8,256,256]{2,1,0:T(8,128)(2,1)S(1)}, bf16[8,256,256]{2,1,0:T(8,128)(2,1)S(1)}, u32[]{:S(2)}, u32[]{:S(2)}) collective-permute-start(bf16[8,256,256]{2,1,0:T(8,128)(2,1)S(1)} %all_to_all.15.same), channel_id=1, source_target_pairs={{0,8},{8,0},{16,24},{24,16},{32,40},{40,32},{48,56},{56,48},{64,72... | collective-permute-start | bytes 3145736 | tf_op jit(solution)/shard_map/ppermute | solution.py:459
  25.0 1.7 %copy-start.3 = (s32[272,2]{0,1:T(2,128)S(1)}, s32[272,2]{0,1:T(2,128)}, u32[]{:S(2)}) copy-start(s32[272,2]{0,1:T(2,128)} %param.11) | copy-start | bytes 6532
  25.1 2.0 %copy-start.2 = (bf16[8,128,128]{2,1,0:T(8,128)(2,1)S(1)}, bf16[8,128,128]{2,1,0:T(8,128)(2,1)}, u32[]{:S(2)}) copy-start(bf16[8,128,128]{2,1,0:T(8,128)(2,1)} %param.9) | copy-start | bytes 786436
  25.1 10.1 %collective-permute-start.1 = (bf16[8,128,128]{2,1,0:T(8,128)(2,1)S(1)}, bf16[8,128,128]{2,1,0:T(8,128)(2,1)S(1)}, u32[]{:S(2)}, u32[]{:S(2)}) collective-permute-start(bf16[8,128,128]{2,1,0:T(8,128)(2,1)S(1)} %bitcast.17), channel_id=1, source_target_pairs={{0,120},{8,112},{16,104},{24,96},{32,88},{40,80},{48,72},{56,64},{... | collective-permute-start | bytes 786440 | tf_op jit(solution)/shard_map/ppermute | solution.py:463
  27.3 7.9 %copy-start = (bf16[1,128,128]{2,1,0:T(8,128)(2,1)S(1)}, bf16[1,128,128]{2,1,0:T(8,128)(2,1)}, u32[]{:S(2)}) copy-start(bf16[1,128,128]{2,1,0:T(8,128)(2,1)} %param.10) | copy-start | bytes 98308
  49.5 1.6 %collective-permute-start.2 = (bf16[8,80,128]{2,1,0:T(8,128)(2,1)S(1)}, bf16[8,80,128]{2,1,0:T(8,128)(2,1)S(1)}, u32[]{:S(2)}, u32[]{:S(2)}) collective-permute-start(bf16[8,80,128]{2,1,0:T(8,128)(2,1)S(1)} %get-tuple-element.11), channel_id=1, source_target_pairs={{0,8},{8,0},{16,24},{24,16},{32,40},{40,32},{48,56},{56,48},{64,72... | collective-permute-start | bytes 491528 | tf_op jit(solution)/shard_map/ppermute | solution.py:477
  60.8 3.9 %collective-permute-start.4 = (bf16[72,128]{1,0:T(8,128)(2,1)S(1)}, bf16[72,128]{1,0:T(8,128)(2,1)S(1)}, u32[]{:S(2)}, u32[]{:S(2)}) collective-permute-start(bf16[72,128]{1,0:T(8,128)(2,1)S(1)} %get-tuple-element.13), channel_id=1, source_target_pairs={{0,8},{8,0},{16,24},{24,16},{32,40},{40,32},{48,56},{56,48},{64,72... | collective-permute-start | bytes 55304 | tf_op jit(solution)/shard_map/ppermute | solution.py:490
  60.9 3.8 %collective-permute-start.3 = (bf16[72,128]{1,0:T(8,128)(2,1)S(1)}, bf16[72,128]{1,0:T(8,128)(2,1)S(1)}, u32[]{:S(2)}, u32[]{:S(2)}) collective-permute-start(bf16[72,128]{1,0:T(8,128)(2,1)S(1)} %get-tuple-element.13), channel_id=1, source_target_pairs={{0,16},{8,24},{16,0},{24,8},{32,48},{40,56},{48,32},{56,40},{64,80... | collective-permute-start | bytes 55304 | tf_op jit(solution)/shard_map/ppermute | solution.py:489
  64.8 1.2 %collective-permute-start.5 = (bf16[72,128]{1,0:T(8,128)(2,1)S(1)}, bf16[72,128]{1,0:T(8,128)(2,1)S(1)}, u32[]{:S(2)}, u32[]{:S(2)}) collective-permute-start(bf16[72,128]{1,0:T(8,128)(2,1)S(1)} %collective-permute-done.3), channel_id=1, source_target_pairs={{0,8},{8,0},{16,24},{24,16},{32,40},{40,32},{48,56},{56,48},{64,72... | collective-permute-start | bytes 55304 | tf_op jit(solution)/shard_map/ppermute | solution.py:491
  66.0 22.0 %collective-permute-start.8 = (bf16[288,128]{1,0:T(8,128)(2,1)S(1)}, bf16[288,128]{1,0:T(8,128)(2,1)S(1)}, u32[]{:S(2)}, u32[]{:S(2)}) collective-permute-start(bf16[288,128]{1,0:T(8,128)(2,1)S(1)} %constant_dynamic-update-slice_fusion.layer0), channel_id=1, source_target_pairs={{0,96},{8,104},{16,112},{24,120},{32,0},{40,8},{48,16},{56,24},{64... | collective-permute-start | bytes 221192 | tf_op jit(solution)/shard_map/ppermute | solution.py:493
  66.9 21.1 %collective-permute-start.7 = (bf16[288,128]{1,0:T(8,128)(2,1)S(1)}, bf16[288,128]{1,0:T(8,128)(2,1)S(1)}, u32[]{:S(2)}, u32[]{:S(2)}) collective-permute-start(bf16[288,128]{1,0:T(8,128)(2,1)S(1)} %constant_dynamic-update-slice_fusion.layer0), channel_id=1, source_target_pairs={{0,64},{8,72},{16,80},{24,88},{32,96},{40,104},{48,112},{56,120},{... | collective-permute-start | bytes 221192 | tf_op jit(solution)/shard_map/ppermute | solution.py:493
  68.4 19.6 %collective-permute-start.6 = (bf16[288,128]{1,0:T(8,128)(2,1)S(1)}, bf16[288,128]{1,0:T(8,128)(2,1)S(1)}, u32[]{:S(2)}, u32[]{:S(2)}) collective-permute-start(bf16[288,128]{1,0:T(8,128)(2,1)S(1)} %constant_dynamic-update-slice_fusion.layer0), channel_id=1, source_target_pairs={{0,32},{8,40},{16,48},{24,56},{32,64},{40,72},{48,80},{56,88},{64,... | collective-permute-start | bytes 221192 | tf_op jit(solution)/shard_map/ppermute | solution.py:493

commit v5 on v4

--- a/solution.py
+++ b/solution.py
@@ -141,7 +141,8 @@
         mk[step, :, HD:] = down
         mk_t[step, :HD] = up.T
         mk_t[step, HD:] = down.T
-        v_t[step] = value_rows(step).T
+        v_t[step, :HD] = value_rows(step).T
+        v_t[step, HD:] = jnp.ones((16, 2 * BLK), BF16)
         k_t[step] = keys.T
 
     def allowed_of(side):
@@ -203,28 +204,26 @@
                 m_acc[side, c] = new
                 shift = jnp.exp2((old - new) * shrink)
                 shift_buf[c] = shift
-            total = jnp.zeros((8, wide), F32)
             for row in range(0, 2 * BLK, tile):
                 part = masked(s_buf[pl.ds(row, tile), lanes], row, FLOOR)
                 weights = jnp.exp2((part - new) * shrink)
-                total = total + over_sublanes(weights, jnp.sum)
                 p_buf[pl.ds(row, tile), lanes] = weights.astype(BF16)
-            l_acc[side, c] = total if first else l_acc[side, c] * shift + total
-        for c in range(chunks):
-            lanes = pl.ds(c * wide, wide)
-            total = jnp.zeros((8, wide), F32)
+        for c in range(chunks):
+            lanes = pl.ds(c * wide, wide)
             for row in range(0, 2 * BLK, tile):
                 part = masked(x_raw[pl.ds(row, tile), lanes], row, 0.0)
-                total = total + over_sublanes(part, jnp.sum)
                 x_buf[pl.ds(row, tile), lanes] = part.astype(BF16)
+        for c in range(chunks):
+            lanes = pl.ds(c * wide, wide)
+            product = dot(v_t[step], x_buf[:, lanes])
+            total, product = product[HD : HD + 8], product[:HD]
             n_acc[side, c] = total if first else n_acc[side, c] + total
-        for c in range(chunks):
-            lanes = pl.ds(c * wide, wide)
-            product = dot(v_t[step], x_buf[:, lanes])
             s_acc[side, c] = product if first else s_acc[side, c] + product
         for c in range(chunks):
             lanes = pl.ds(c * wide, wide)
             product = dot(v_t[step], p_buf[:, lanes])
+            total, product = product[HD : HD + 8], product[:HD]
+            l_acc[side, c] = total if first else l_acc[side, c] * shift_buf[c] + total
             t_acc[side, c] = product if first else t_acc[side, c] * shift_buf[c] + product
 
     for slot in range(SLOTS):
@@ -243,9 +242,9 @@
 
     def settle(side, loss):
         for c in range(chunks):
-            norm = 1.0 / jnp.sum(n_acc[side, c], axis=0, keepdims=True)
+            norm = 1.0 / n_acc[side, c][:1]
             student = s_acc[side, c] * norm
-            mass = 1.0 / jnp.sum(l_acc[side, c], axis=0, keepdims=True)
+            mass = 1.0 / l_acc[side, c][:1]
             mismatch = student - t_acc[side, c] * mass
             upstream = 2.0 * mismatch
             gn[side, c] = (upstream * norm).astype(BF16)
@@ -413,7 +412,7 @@
             pltpu.VMEM((2, wide, 2 * HD), BF16),
             pltpu.VMEM((2, 2 * HD, wide), F32),
             pltpu.VMEM((SLOTS, BLK, 2 * HD), BF16),
-            pltpu.VMEM((STEPS, HD, pair), BF16),
+            pltpu.VMEM((STEPS, HD + 16, pair), BF16),
             pltpu.VMEM((STEPS, HD, pair), BF16),
             pltpu.VMEM((STEPS, pair, 2 * HD), F32),
             pltpu.VMEM((STEPS, pair, 2 * HD), BF16),

time: 90.2 us -> 89.5 us (level)
  no operation moved by 1% of the time
where the time goes in v5:
time: 89.5 us; the launch traced here: 88.4 us
  blocking collectives  51.3 us (57%)
  Pallas kernels  21.3 us (24%)
  waiting for transfers between devices  8.57 us (10%)
  starting transfers between devices  5.82 us (7%)
    all_to_all x1, blocking collectives, layer(): lax.all_to_all(sent, 'seq', 0, 0, axis_index_groups=SAME_CORE, tiled=True)  22.4 us
    all_to_all x1, blocking collectives, layer(): stats = lax.all_to_all(stats, ('seq', 'kv'), 0, 0, tiled=True)  19.4 us
    pallas_call x1, Pallas kernels, attend(): pl.pallas_call(main_kernel, out_shape=(shape((CHIPS, PAYLOAD, BLK), F32),...  13.6 us
    all_to_all x1, blocking collectives, layer(): lax.all_to_all(met, 'seq', 0, 0, axis_index_groups=SAME_CORE, tiled=True)  9.5 us
    pallas_call x1, Pallas kernels, layer(): pl.pallas_call(list_kernel, out_shape=shape((128,), jnp.int32), in_specs=...  4.48 us
    ppermute x1, waiting for transfers between devices, layer(): late = lax.ppermute(late, 'seq', MIRROR)  3.4 us
    ppermute x1, waiting for transfers between devices, layer(): across = lax.ppermute(chunk, 'seq', OTHER_ROW)  2.97 us
    ppermute x3, starting transfers between devices, layer(): lax.ppermute(near, 'seq', route)  2.6 us
  transfers between devices with their start and end apart: 9, of which 4 were waited for; matrix products, arithmetic and copies ran while one was open for 1% of the time, Pallas kernels for 5%

profile of v5, /device:TPU:0, one launch (start us, length us, event | category | flops | bytes accessed | tf_op | source)
XLA Modules:
  0.0 88.4 jit_solution(15412525151574471632)
XLA Ops:
  0.6 1.9 %pack.1 = bf16[8,256,256]{2,1,0:T(8,128)(2,1)} custom-call(bf16[256,128]{1,0:T(8,128)(2,1)} %bitcast.18, bf16[256,128]{1,0:T(8,128)(2,1)} %bitcast.19), custom_call_target="tpu_custom_call" | custom-call | tf_op jit(solution)/shard_map/pack/pallas_call | solution.py:445
  2.6 0.0 copy-start.1
  2.6 22.4 %all_to_all.15.same = bf16[8,256,256]{2,1,0:T(8,128)(2,1)S(1)} all-to-all(bf16[8,256,256]{2,1,0:T(8,128)(2,1)} %pack.1), channel_id=1, replica_groups={{0,16,32,48,64,80,96,112},{8,24,40,56,72,88,104,120},{1,17,33,49,65,81,..., dimensions={0} | all-to-all | bytes 2097152 | tf_op jit(solution)/shard_map/all_to_all | solution.py:457
  25.0 0.0 collective-permute-start
  25.0 0.0 copy-start.3
  25.1 0.0 copy-start.2
  25.1 1.7 %collective-permute-start.1 = (bf16[8,128,128]{2,1,0:T(8,128)(2,1)S(1)}, bf16[8,128,128]{2,1,0:T(8,128)(2,1)S(1)}, u32[]{:S(2)}, u32[]{:S(2)}) collective-permute-start(bf16[8,128,128]{2,1,0:T(8,128)(2,1)S(1)} %bitcast.17), channel_id=1, source_target_pairs={{0,120},{8,112},{16,104},{24,96},{32,88},{40,80},{48,72},{56,64},{... | collective-permute-start | bytes 786440 | tf_op jit(solution)/shard_map/ppermute | solution.py:462
  26.8 0.1 copy.12
  26.9 0.1 reshape.22.pairs
  27.1 0.2 copy.15
  27.3 0.0 copy-start
  27.3 4.5 %list.1.info = s32[128]{0:T(128)S(1)} custom-call(s32[1]{0:T(128)} %bitcast.place, s32[544]{0:T(1024)S(1)} %reshape.22.pairs), custom_call_target="tpu_custom_call" | custom-call | flops 5000000000 | bytes 100000 | tf_op jit(solution)/shard_map/list/pallas_call | solution.py:464
  31.8 3.4 %collective-permute-done.1.late = bf16[8,128,128]{2,1,0:T(8,128)(2,1)S(1)} collective-permute-done((bf16[8,128,128]{2,1,0:T(8,128)(2,1)S(1)}, bf16[8,128,128]{2,1,0:T(8,128)(2,1)S(1)}, u32[]{:S(2)}, u32[]{:S(2)}) %collective-permute-start.1) | collective-permute-done | bytes 262176 | tf_op jit(solution)/shard_map/ppermute | solution.py:462
  35.2 0.0 collective-permute-done.other
  35.2 13.6 %attend.1 = (f32[8,80,128]{2,1,0:T(8,128)S(1)}, bf16[8,80,128]{2,1,0:T(8,128)(2,1)S(1)}) custom-call(s32[128]{0:T(128)S(1)} %list.1.info, bf16[8,256,256]{2,1,0:T(8,128)(2,1)S(1)} %all_to_all.15.same, bf16[8,256,256]{2,1,0:T(8,128)(2,1)S(1)} %collective-permute-done.other, bf16[128,128]{1,0:T(8,128)(2,1)S(1)} %bitcast.16, bf16[8,128,128]{2,1,0:T(8,128)(2,1)S(1)} %bitcast.15, ...), custom_call_target="tpu_custom_call" | custom-call | tf_op jit(solution)/shard_map/attend/pallas_call | solution.py:404
  48.8 0.6 collective-permute-start.2
  49.4 1.0 %collective-permute-done.2 = bf16[8,80,128]{2,1,0:T(8,128)(2,1)S(1)} collective-permute-done((bf16[8,80,128]{2,1,0:T(8,128)(2,1)S(1)}, bf16[8,80,128]{2,1,0:T(8,128)(2,1)S(1)}, u32[]{:S(2)}, u32[]{:S(2)}) %collective-permute-start.2) | collective-permute-done | bytes 163872 | tf_op jit(solution)/shard_map/ppermute | solution.py:476
  50.5 9.5 %all_to_all.16.pieces = bf16[8,80,128]{2,1,0:T(8,128)(2,1)S(1)} all-to-all(bf16[8,80,128]{2,1,0:T(8,128)(2,1)S(1)} %add_convert_fusion), channel_id=1, replica_groups={{0,16,32,48,64,80,96,112},{8,24,40,56,72,88,104,120},{1,17,33,49,65,81,..., dimensions={0} | all-to-all | bytes 327680 | tf_op jit(solution)/shard_map/all_to_all | solution.py:477
  60.0 0.2 fold.1
  60.1 0.1 collective-permute-start.4
  60.2 0.9 collective-permute-start.3
  61.1 3.0 %collective-permute-done.3 = bf16[72,128]{1,0:T(8,128)(2,1)S(1)} collective-permute-done((bf16[72,128]{1,0:T(8,128)(2,1)S(1)}, bf16[72,128]{1,0:T(8,128)(2,1)S(1)}, u32[]{:S(2)}, u32[]{:S(2)}) %collective-permute-start.3) | collective-permute-done | bytes 18464 | tf_op jit(solution)/shard_map/ppermute | solution.py:488
  64.1 0.0 collective-permute-start.5
  64.1 0.0 collective-permute-done.4
  64.1 1.2 %collective-permute-done.5 = bf16[72,128]{1,0:T(8,128)(2,1)S(1)} collective-permute-done((bf16[72,128]{1,0:T(8,128)(2,1)S(1)}, bf16[72,128]{1,0:T(8,128)(2,1)S(1)}, u32[]{:S(2)}, u32[]{:S(2)}) %collective-permute-start.5) | collective-permute-done | bytes 18464 | tf_op jit(solution)/shard_map/ppermute | solution.py:490
  65.3 0.9 %collective-permute-start.8 = (bf16[288,128]{1,0:T(8,128)(2,1)S(1)}, bf16[288,128]{1,0:T(8,128)(2,1)S(1)}, u32[]{:S(2)}, u32[]{:S(2)}) collective-permute-start(bf16[288,128]{1,0:T(8,128)(2,1)S(1)} %constant_dynamic-update-slice_fusion.layer0), channel_id=1, source_target_pairs={{0,96},{8,104},{16,112},{24,120},{32,0},{40,8},{48,16},{56,24},{64... | collective-permute-start | bytes 221192 | tf_op jit(solution)/shard_map/ppermute | solution.py:492
  66.2 1.5 %collective-permute-start.7 = (bf16[288,128]{1,0:T(8,128)(2,1)S(1)}, bf16[288,128]{1,0:T(8,128)(2,1)S(1)}, u32[]{:S(2)}, u32[]{:S(2)}) collective-permute-start(bf16[288,128]{1,0:T(8,128)(2,1)S(1)} %constant_dynamic-update-slice_fusion.layer0), channel_id=1, source_target_pairs={{0,64},{8,72},{16,80},{24,88},{32,96},{40,104},{48,112},{56,120},{... | collective-permute-start | bytes 221192 | tf_op jit(solution)/shard_map/ppermute | solution.py:492
  67.7 0.2 collective-permute-start.6
  67.9 19.4 %all_to_all.17.stats = f32[128,1,128]{2,1,0:T(1,128)S(1)} all-to-all(f32[128,1,128]{2,1,0:T(1,128)S(1)} %get-tuple-element.12), channel_id=1, replica_groups=mesh['seq'=16,'kv'=8] {'seq','kv'}, dimensions={0} | all-to-all | bytes 131072 | tf_op jit(solution)/shard_map/all_to_all | solution.py:487
  87.3 0.0 collective-permute-done.8.layer3
  87.3 0.0 collective-permute-done.6.layer1
  87.3 1.1 %scale.1 = (f32[1024,128]{1,0:T(8,128)}, f32[128,128]{1,0:T(8,128)}, f32[1,1]{1,0:T(1,128)}) custom-call(s32[1]{0:T(128)} %bitcast.place, f32[128,1,128]{2,1,0:T(1,128)S(1)} %all_to_all.17.stats, bf16[288,128]{1,0:T(8,128)(2,1)S(1)} %constant_dynamic-update-slice_fusion.layer0, bf16[288,128]{1,0:T(8,128)(2,1)S(1)} %collective-permute-done.6.layer1, ...), custom_call_target="tpu_custom_call" | custom-call | tf_op jit(solution)/shard_map/scale/pallas_call | solution.py:493
  (13 shorter events, 0.2 us)
Async XLA Ops:
  2.6 22.4 %copy-start.1 = (bf16[256,8,128]{2,1,0:T(8,128)(2,1)S(1)}, bf16[256,8,128]{2,1,0:T(8,128)(2,1)}, u32[]{:S(2)}) copy-start(bf16[256,8,128]{2,1,0:T(8,128)(2,1)} %param.6) | copy-start | bytes 1572868
  25.0 10.2 %collective-permute-start = (bf16[8,256,256]{2,1,0:T(8,128)(2,1)S(1)}, bf16[8,256,256]{2,1,0:T(8,128)(2,1)S(1)}, u32[]{:S(2)}, u32[]{:S(2)}) collective-permute-start(bf16[8,256,256]{2,1,0:T(8,128)(2,1)S(1)} %all_to_all.15.same), channel_id=1, source_target_pairs={{0,8},{8,0},{16,24},{24,16},{32,40},{40,32},{48,56},{56,48},{64,72... | collective-permute-start | bytes 3145736 | tf_op jit(solution)/shard_map/ppermute | solution.py:458
  25.0 1.7 %copy-start.3 = (s32[272,2]{0,1:T(2,128)S(1)}, s32[272,2]{0,1:T(2,128)}, u32[]{:S(2)}) copy-start(s32[272,2]{0,1:T(2,128)} %param.11) | copy-start | bytes 6532
  25.1 2.0 %copy-start.2 = (bf16[8,128,128]{2,1,0:T(8,128)(2,1)S(1)}, bf16[8,128,128]{2,1,0:T(8,128)(2,1)}, u32[]{:S(2)}) copy-start(bf16[8,128,128]{2,1,0:T(8,128)(2,1)} %param.9) | copy-start | bytes 786436
  25.1 10.1 %collective-permute-start.1 = (bf16[8,128,128]{2,1,0:T(8,128)(2,1)S(1)}, bf16[8,128,128]{2,1,0:T(8,128)(2,1)S(1)}, u32[]{:S(2)}, u32[]{:S(2)}) collective-permute-start(bf16[8,128,128]{2,1,0:T(8,128)(2,1)S(1)} %bitcast.17), channel_id=1, source_target_pairs={{0,120},{8,112},{16,104},{24,96},{32,88},{40,80},{48,72},{56,64},{... | collective-permute-start | bytes 786440 | tf_op jit(solution)/shard_map/ppermute | solution.py:462
  27.3 7.9 %copy-start = (bf16[1,128,128]{2,1,0:T(8,128)(2,1)S(1)}, bf16[1,128,128]{2,1,0:T(8,128)(2,1)}, u32[]{:S(2)}) copy-start(bf16[1,128,128]{2,1,0:T(8,128)(2,1)} %param.10) | copy-start | bytes 98308
  48.8 1.6 %collective-permute-start.2 = (bf16[8,80,128]{2,1,0:T(8,128)(2,1)S(1)}, bf16[8,80,128]{2,1,0:T(8,128)(2,1)S(1)}, u32[]{:S(2)}, u32[]{:S(2)}) collective-permute-start(bf16[8,80,128]{2,1,0:T(8,128)(2,1)S(1)} %get-tuple-element.11), channel_id=1, source_target_pairs={{0,8},{8,0},{16,24},{24,16},{32,40},{40,32},{48,56},{56,48},{64,72... | collective-permute-start | bytes 491528 | tf_op jit(solution)/shard_map/ppermute | solution.py:476
  60.1 3.9 %collective-permute-start.4 = (bf16[72,128]{1,0:T(8,128)(2,1)S(1)}, bf16[72,128]{1,0:T(8,128)(2,1)S(1)}, u32[]{:S(2)}, u32[]{:S(2)}) collective-permute-start(bf16[72,128]{1,0:T(8,128)(2,1)S(1)} %get-tuple-element.13), channel_id=1, source_target_pairs={{0,8},{8,0},{16,24},{24,16},{32,40},{40,32},{48,56},{56,48},{64,72... | collective-permute-start | bytes 55304 | tf_op jit(solution)/shard_map/ppermute | solution.py:489
  60.2 3.8 %collective-permute-start.3 = (bf16[72,128]{1,0:T(8,128)(2,1)S(1)}, bf16[72,128]{1,0:T(8,128)(2,1)S(1)}, u32[]{:S(2)}, u32[]{:S(2)}) collective-permute-start(bf16[72,128]{1,0:T(8,128)(2,1)S(1)} %get-tuple-element.13), channel_id=1, source_target_pairs={{0,16},{8,24},{16,0},{24,8},{32,48},{40,56},{48,32},{56,40},{64,80... | collective-permute-start | bytes 55304 | tf_op jit(solution)/shard_map/ppermute | solution.py:488
  64.1 1.2 %collective-permute-start.5 = (bf16[72,128]{1,0:T(8,128)(2,1)S(1)}, bf16[72,128]{1,0:T(8,128)(2,1)S(1)}, u32[]{:S(2)}, u32[]{:S(2)}) collective-permute-start(bf16[72,128]{1,0:T(8,128)(2,1)S(1)} %collective-permute-done.3), channel_id=1, source_target_pairs={{0,8},{8,0},{16,24},{24,16},{32,40},{40,32},{48,56},{56,48},{64,72... | collective-permute-start | bytes 55304 | tf_op jit(solution)/shard_map/ppermute | solution.py:490
  65.3 22.0 %collective-permute-start.8 = (bf16[288,128]{1,0:T(8,128)(2,1)S(1)}, bf16[288,128]{1,0:T(8,128)(2,1)S(1)}, u32[]{:S(2)}, u32[]{:S(2)}) collective-permute-start(bf16[288,128]{1,0:T(8,128)(2,1)S(1)} %constant_dynamic-update-slice_fusion.layer0), channel_id=1, source_target_pairs={{0,96},{8,104},{16,112},{24,120},{32,0},{40,8},{48,16},{56,24},{64... | collective-permute-start | bytes 221192 | tf_op jit(solution)/shard_map/ppermute | solution.py:492
  66.2 21.1 %collective-permute-start.7 = (bf16[288,128]{1,0:T(8,128)(2,1)S(1)}, bf16[288,128]{1,0:T(8,128)(2,1)S(1)}, u32[]{:S(2)}, u32[]{:S(2)}) collective-permute-start(bf16[288,128]{1,0:T(8,128)(2,1)S(1)} %constant_dynamic-update-slice_fusion.layer0), channel_id=1, source_target_pairs={{0,64},{8,72},{16,80},{24,88},{32,96},{40,104},{48,112},{56,120},{... | collective-permute-start | bytes 221192 | tf_op jit(solution)/shard_map/ppermute | solution.py:492
  67.7 19.6 %collective-permute-start.6 = (bf16[288,128]{1,0:T(8,128)(2,1)S(1)}, bf16[288,128]{1,0:T(8,128)(2,1)S(1)}, u32[]{:S(2)}, u32[]{:S(2)}) collective-permute-start(bf16[288,128]{1,0:T(8,128)(2,1)S(1)} %constant_dynamic-update-slice_fusion.layer0), channel_id=1, source_target_pairs={{0,32},{8,40},{16,48},{24,56},{32,64},{40,72},{48,80},{56,88},{64,... | collective-permute-start | bytes 221192 | tf_op jit(solution)/shard_map/ppermute | solution.py:492
